TPU v7x, 512 devices: a whole 4x8x8 slice. The times are simulated.
512 devices in a mesh: row: 64 (over z, y), col: 8 (over x, core).
Axes of the slice: x: 4, y: 8, z: 8, core: 2. Of those that a mesh axis runs over, the one named last changes fastest.
Arguments:
- left_site: bfloat16 [1536, 3, 4096], P('row'), may hold values from -6 to 6
- right_site: bfloat16 [4096, 3, 4096], P('row', None, 'col'), may hold values from -0.09375 to 0.09375
- gate: float32 [9, 9], replicated, may hold values from -2 to 2
- probes_matrix: bfloat16 [12288, 256], P('col'), may hold values from -0.0546875 to 0.0546875
Outputs:
- basis: float32 [4608, 256], P('row')
- new_block: float32 [256, 12288], P('row', 'col')
All inputs are finite; a program needn't handle non-finite values.
Results may differ from a plain program's by a relative error of at most 0.0044.
Values may be sent and summed in bfloat16 or wider, within the bound.
No kernel may reach another device: no remote copies, remote signals or barrier semaphores. Data moves between devices by JAX's collectives and lax.ppermute only.
A program may use at most 128 MiB of HBM per device.

v0:
```python
import jax
import jax.numpy as jnp
from jax import lax
from jax.sharding import PartitionSpec as P

CUTOFF = 3


def total_of_pieces(shard, axis):
    return lax.all_gather(shard, axis).sum(0)


def local(left_site, right_site, gate, probes_matrix):
    count_a = left_site.shape[0]
    bond = left_site.shape[2]
    width_b = right_site.shape[2]
    left_rows = left_site.reshape(count_a * CUTOFF, bond)
    gate_four = gate.reshape(CUTOFF, CUTOFF, CUTOFF, CUTOFF)
    place = lax.axis_index("row")
    piece = lax.all_gather(right_site, "row", axis=0, tiled=True)
    depth = piece.shape[0]
    mixed = jnp.dot(
        left_rows, piece.reshape(depth, CUTOFF * width_b), preferred_element_type=jnp.float32
    )
    mixed = mixed.reshape(count_a, CUTOFF, CUTOFF, width_b)
    theta = jnp.einsum("stuv,auvb->asbt", gate_four, mixed, precision=lax.Precision.HIGHEST)
    theta = theta.reshape(count_a * CUTOFF, width_b * CUTOFF).astype(jnp.bfloat16)
    partial_value = jnp.dot(theta, probes_matrix, preferred_element_type=jnp.float32)
    total = total_of_pieces(partial_value, "col")
    sketch_tile = total.astype(jnp.bfloat16)
    probes = sketch_tile.shape[1]
    gram_part = lax.dot_general(
        sketch_tile, sketch_tile, (((0,), (0,)), ((), ())), preferred_element_type=jnp.float32
    )
    sketch_wide = sketch_tile.astype(jnp.float32)
    projected_tile = lax.dot_general(
        sketch_tile, theta, (((0,), (0,)), ((), ())), preferred_element_type=jnp.float32
    )
    gram, projected = lax.psum((gram_part, projected_tile), "row")
    factor = jnp.linalg.cholesky(gram)
    basis = lax.linalg.triangular_solve(
        factor, sketch_wide, left_side=False, lower=True, transpose_a=True
    )
    solved = lax.linalg.triangular_solve(factor, projected, left_side=True, lower=True)
    own_rows = probes // lax.axis_size("row")
    new_block = lax.dynamic_slice_in_dim(solved, place * own_rows, own_rows, 0)
    return (basis, new_block)


def solution(mesh):
    return jax.shard_map(
        local,
        mesh=mesh,
        in_specs=(P("row", None, None), P("row", None, "col"), P(), P("col", None)),
        out_specs=(P("row", None), P("row", "col")),
        check_vma=False,
    )
```

profile of v0, /device:TPU:2, one launch (start us, length us, event | category | flops | bytes accessed | tf_op | source)
XLA Modules:
  0.0 430.8 jit_solution(5389747223145043462)
XLA Ops:
  7.2 0.7 all-gather.3.cloned.1.call-update
  8.0 0.8 reshape.39
  8.7 126.3 %all-gather.3.cloned.1.call-done = bf16[4096,3,512]{2,0,1:T(8,128)(2,1)} async-done(((bf16[64,3,512]{2,0,1:T(8,128)(2,1)}), bf16[4096,3,512]{2,0,1:T(8,128)(2,1)}) %all-gather.3.cloned.1.call-update) | async-done | bytes 12582928 | tf_op jit(solution)/shard_map/all_gather | solution.py:20
  135.0 17.0 %copy.14 = bf16[4096,3,512]{0,2,1:T(8,128)(2,1)} copy(bf16[4096,3,512]{2,0,1:T(8,128)(2,1)} %all-gather.3.cloned.1.call-done) | data formatting | bytes 25165824 | tf_op jit(solution)/shard_map/all_gather | solution.py:20
  152.0 8.5 %fusion.3 = f32[24,3,3,512,1]{3,0,2,1,4:T(8,128)S(1)} fusion(bf16[4096,3,512]{0,2,1:T(8,128)(2,1)} %copy.14, bf16[24,3,4096]{2,0,1:T(8,128)(2,1)S(1)} %copy-done.2), kind=kOutput, calls=%fused_computation.9 | convolution fusion | flops 905969664 | bytes 13615104 | tf_op jit(solution)/shard_map/dot_general | solution.py:22
  160.5 1.4 fusion.6
  161.9 6.5 %copy.17 = bf16[24,3,512,3]{3,2,1,0:T(8,128)(2,1)} copy(bf16[24,3,512,3]{2,3,1,0:T(4,128)(2,1)S(1)} %fusion.6) | data formatting | bytes 442368 | tf_op jit(solution)/shard_map/convert_element_type | solution.py:27
  168.4 11.9 %convert_element_type.15 = bf16[72,1536]{1,0:T(8,128)(2,1)S(1)} reshape(bf16[24,3,512,3]{3,2,1,0:T(8,128)(2,1)} %copy.17) | data formatting | bytes 442368 | tf_op jit(solution)/shard_map/convert_element_type | solution.py:27
  180.6 13.4 %all-gather = f32[576,256]{1,0:T(8,128)S(1)} all-gather(f32[72,256]{1,0:T(8,128)S(1)} %fusion.25), channel_id=2, replica_groups=mesh['row'=64,'col'=8] {'col'}, dimensions={0}, use_global_device_ids=true | all-gather | bytes 663552 | tf_op jit(solution)/shard_map/all_gather | solution.py:10
  194.0 1.5 fusion.27
  195.5 0.9 fusion.26
  196.5 161.3 %all-reduce.4.cloned.1.call-done = (f32[256,256]{0,1:T(8,128)}, f32[256,1536]{1,0:T(8,128)}) async-done(((f32[256,256]{0,1:T(8,128)}, f32[256,1536]{1,0:T(8,128)}), (f32[256,256]{0,1:T(8,128)}, f32[256,1536]{1,0:T(8,128)})) %all-reduce.4.cloned.1.call-update) | async-done | bytes 1835024 | tf_op jit(solution)/shard_map/psum | solution.py:39
  357.8 1.1 copy.19
  358.9 1.0 fusion.11
  359.9 11.7 %cholesky.50 = f32[128,128]{1,0:T(8,128)S(1)} custom-call(f32[128,128]{1,0:T(8,128)S(1)} %cholesky.118), custom_call_target="Cholesky" | custom-call | tf_op jit(solution)/shard_map/jit(cholesky)/cholesky | solution.py:40
  371.7 9.8 %custom-call.16 = f32[1,128,128]{1,2,0:T(8,128)S(1)} custom-call(f32[1,128,128]{2,1,0:T(8,128)S(1)} %get-tuple-element.25), custom_call_target="InvertDiagBlocksLowerTriangular" | custom-call | tf_op jit(solution)/shard_map/jit(cholesky)/cholesky | solution.py:40
  382.0 11.7 %cholesky.105 = f32[128,128]{1,0:T(8,128)S(1)} custom-call(f32[128,128]{1,0:T(8,128)S(1)} %convolution_subtract_fusion.1), custom_call_target="Cholesky" | custom-call | tf_op jit(solution)/shard_map/jit(cholesky)/cholesky | solution.py:40
  395.8 4.1 while.1
  396.6 1.3 bitcast_dynamic-update-slice_fusion.2
  398.5 1.3 bitcast_dynamic-update-slice_fusion.2
  399.9 19.7 %custom-call.17 = f32[2,128,128]{1,2,0:T(8,128)S(1)} custom-call(f32[2,128,128]{2,1,0:T(8,128)S(1)} %get-tuple-element.9), custom_call_target="InvertDiagBlocksLowerTriangular" | custom-call | tf_op jit(solution)/shard_map/triangular_solve | solution.py:41
  419.7 0.8 fusion.7
  420.6 0.8 convolution_subtract_fusion
  421.4 0.8 fusion.16
  (31 shorter events, 4.9 us)
Async XLA Ops:
  7.2 173.1 %copy-start = (bf16[1536,256]{1,0:T(8,128)(2,1)S(1)}, bf16[1536,256]{1,0:T(8,128)(2,1)}, u32[]{:S(2)}) copy-start(bf16[1536,256]{1,0:T(8,128)(2,1)} %param.7) | copy-start | bytes 2359300
  7.2 127.8 %all-gather.3.cloned.1.call-start = ((), (), s32[]{:S(2)}) async-start(), calls=%async_computation | async-start | bytes 12779520 | tf_op jit(solution)/shard_map/all_gather | solution.py:20
  7.9 349.9 %all-reduce.4.cloned.1.call-start = ((), (), s32[]{:S(2)}) async-start(), calls=%async_computation.1 | async-start | bytes 3670016 | tf_op jit(solution)/shard_map/psum | solution.py:39
  8.7 143.3 %copy-start.2 = (bf16[24,3,4096]{2,0,1:T(8,128)(2,1)S(1)}, bf16[24,3,4096]{2,0,1:T(8,128)(2,1)}, u32[]{:S(2)}) copy-start(bf16[24,3,4096]{2,0,1:T(8,128)(2,1)} %param.4) | copy-start | bytes 1769476
  359.9 59.8 %copy-start.1 = (f32[256,1536]{1,0:T(8,128)S(1)}, f32[256,1536]{1,0:T(8,128)}, u32[]{:S(2)}) copy-start(f32[256,1536]{1,0:T(8,128)} %get-tuple-element.19) | copy-start | bytes 4718596
Sparse Core Ops, SparseCore 0:
  11.0 123.9 all-gather.2
  196.6 161.1 all-reduce.3
where the time goes:
time: 432 us; the launch traced here: 431 us
  waiting for transfers between devices  288 us (67%)
  other arithmetic  56 us (13%)
  local copies, waits for them, and re-layouts  41.2 us (10%)
  matrix products  16.2 us (4%)
  between operations  15.5 us (4%)
  blocking collectives  13.4 us (3%)
    psum x1, waiting for transfers between devices, local(): gram, projected = lax.psum((gram_part, projected_tile), 'row')  161 us
    all_gather x1, waiting for transfers between devices, local(): piece = lax.all_gather(right_site, 'row', axis=0, tiled=True)  126 us
    another operation x6, other arithmetic, local(): factor = jnp.linalg.cholesky(gram)  34 us
    another operation x4, other arithmetic, local(): lax.linalg.triangular_solve(factor, sketch_wide, left_side=False, lower=T...  20.4 us
    convert_element_type x2, local copies, waits for them, and re-layouts, local(): theta.reshape(count_a * CUTOFF, width_b * CUTOFF).astype(jnp.bfloat16)  18.4 us
    all_gather x1, local copies, waits for them, and re-layouts, local(): piece = lax.all_gather(right_site, 'row', axis=0, tiled=True)  17 us
    all_gather x1, blocking collectives, total_of_pieces(): return lax.all_gather(shard, axis).sum(0)  13.4 us
  transfers between devices with their start and end apart: 2, of which 2 were waited for; matrix products, arithmetic and copies ran while one was open for 0% of the time, Pallas kernels for 0%

commit v1 on v0

v1 whole, which is shorter than its diff:
```python
import jax
import jax.numpy as jnp
from jax import lax
from jax.experimental import pallas as pl
from jax.experimental.pallas import tpu as pltpu
from jax.sharding import PartitionSpec as P


F32 = jnp.float32
BF16 = jnp.bfloat16
HIGHEST = lax.Precision.HIGHEST
ROWS = 64
COLS = 8


def iota(shape, axis):
    return lax.broadcasted_iota(jnp.int32, shape, axis)


def dot(a, b, dims=((1,), (0,)), precision=None):
    return lax.dot_general(a, b, (dims, ((), ())), precision=precision, preferred_element_type=F32)


def stride_three(t, transposed):
    shape = (384, 128) if transposed else (128, 384)
    b, column = iota(shape, int(transposed)), iota(shape, int(not transposed))
    return jnp.where(column == 3 * b + t, 1.0, 0.0).astype(BF16)


def left_kernel(place, left, left_out, lines):
    row, column, lane = iota((16, 72), 0), iota((16, 72), 1), iota((16, 128), 1)
    sides = []
    for h in range(2):
        line = 2 * row + h
        photon = jnp.where(line < 6, 0, jnp.where(line < 12, 1, 2))
        chosen = (column == photon * 24 + 6 * (place[1] // 2) + line - 6 * photon) & (line < 18)
        sides.append(dot(jnp.where(chosen, 1.0, 0.0).astype(BF16), left[...].reshape(72, 4096)))
    for pair in range(ROWS // 2):
        even, odd = (side[:, 128 * pair : 128 * pair + 128] for side in sides)
        first = jnp.where(lane < 64, even, pltpu.roll(odd, 64, 1))
        second = jnp.where(lane < 64, pltpu.roll(even, 64, 1), odd)
        lines[20 * pair : 20 * pair + 10, :] = first[:10]
        lines[20 * pair + 10 : 20 * pair + 20, :] = second[:10]
    left_out[...] = lines[...].astype(BF16)


def first_kernel(gate, right, probes, weight_out, product):
    wide = right[...].reshape(192, 512)
    for t in range(3):
        pick = stride_three(t, False)
        own = jnp.concatenate(
            [dot(pick, probes[384 * j : 384 * j + 384, :]).astype(BF16) for j in range(4)], axis=0
        )
        product[t] = dot(wide, own)
    for up in range(3):
        for s in range(3):
            total = jnp.zeros((64, 256), F32)
            for tp in range(3):
                for t in range(3):
                    total = total + gate[3 * s + t, 3 * up + tp] * product[t, 64 * tp : 64 * tp + 64, :]
            for core in range(2):
                half = total[:, 128 * core : 128 * core + 128]
                weight_out[core, 64 * up : 64 * up + 64, 128 * s : 128 * s + 128] = half


def weight_kernel(pieces, out):
    total = (pieces[0] + pieces[1]).astype(BF16)
    for x in range(4):
        out[x] = total


def sketch_kernel(left_in, weight, sketch_out, left_rows, wide_left, high, low, wide_sketch):
    wide_left[...] = left_in[...].astype(F32)
    side = iota((64, 128), 1) // 64
    for up in range(3):
        for i in range(6):
            line = 6 * up + i
            tile = jnp.where(side == line % 2, wide_left[pl.ds(line // 2, 64, stride=10), :], 0.0)
            left_rows[64 * i : 64 * i + 64, 128 * up : 128 * up + 128] = tile.astype(BF16)
    total = (weight[0].astype(F32) + weight[1].astype(F32)) + (weight[2].astype(F32) + weight[3].astype(F32))
    for part, wide in zip(split(total), (high, low)):
        for up in range(3):
            block = part[64 * up : 64 * up + 64]
            wide[128 * up : 128 * up + 64, :] = block
            wide[128 * up + 64 : 128 * up + 128, :] = block
    for i in range(6):
        rows = left_rows[64 * i : 64 * i + 64, :]
        part = dot(rows, high[...]) + dot(rows, low[...])
        for s in range(3):
            wide_sketch[pl.ds(3 * i + s, 64, stride=18), :] = part[:, 128 * s : 128 * s + 128]
    sketch_out[...] = wide_sketch[...].astype(BF16)


def total_kernel(pieces, own, out, four, many):
    total = pieces[:144, :].astype(F32)
    for k in range(1, 8):
        total = total + pieces[144 * k : 144 * k + 144, :].astype(F32)
    four[...] = total[:72] + total[72:]
    total = four[0:18, :] + four[18:36, :] + four[36:54, :] + four[54:72, :]
    own[:18, :] = total.astype(BF16)
    own[18:, :] = jnp.zeros((6, 128), BF16)
    for k in range(8):
        many[18 * k : 18 * k + 18, :] = total
    total = many[...].astype(BF16)
    for k in range(8):
        out[144 * k : 144 * k + 144, :] = total


def projection_kernel(place, gate, sketch_in, other_in, left_rows, own, out, wide_sketch, sketch, product, cross):
    core = place[1] % 2
    wide_sketch[...] = sketch_in[...].astype(F32)
    for i in range(6):
        for s in range(3):
            tile = wide_sketch[pl.ds(3 * i + s, 64, stride=18), :]
            sketch[64 * i : 64 * i + 64, 128 * s : 128 * s + 128] = tile.astype(BF16)
    for up in range(3):
        part = dot(left_rows[:, 128 * up : 128 * up + 128], sketch[...], ((0,), (0,)))
        product[64 * up : 64 * up + 64, :] = part[:64] + part[64:]
    for tp in range(3):
        for t in range(3):
            total = jnp.zeros((64, 128), F32)
            for up in range(3):
                for s in range(3):
                    part = product[64 * up : 64 * up + 64, 128 * s : 128 * s + 128]
                    total = total + gate[3 * s + t, 3 * up + tp] * part
            line = 64 * (3 * tp + t)
            total = total.astype(BF16)
            for x in range(4):
                out[x, line : line + 64, :] = total
    mine, other = sketch_in[...], other_in[...]
    block = dot(mine, mine, ((0,), (0,)))
    cross[0] = dot(other, mine, ((0,), (0,)))
    cross[1] = dot(mine, other, ((0,), (0,)))
    half = cross[core, pl.ds(pl.multiple_of(64 * core, 64), 64), :]
    for start, part in ((0, block), (128, half)):
        size = part.shape[0]
        for line, piece in zip((576 + start, 768 + start), split(part)):
            for x in range(4):
                out[x, line : line + size, :] = piece
    for x in range(4):
        out[x, 960:984, :] = own[...]


def middle_kernel(pieces, out):
    total = (pieces[0, :960].astype(F32) + pieces[1, :960].astype(F32)) + (
        pieces[2, :960].astype(F32) + pieces[3, :960].astype(F32)
    )
    value, gram = split(total[:576]), split(total[576:768] + total[768:960])
    for core in range(2):
        out[core, :576, :] = value[0]
        out[core, 576:1152, :] = value[1]
        out[core, 1152:1344, :] = gram[0]
        out[core, 1344:1536, :] = gram[1]
        for x in range(4):
            out[core, 1536 + 24 * x : 1560 + 24 * x, :] = pieces[x, 960:984, :]


def split(value):
    high = value.astype(BF16)
    return high, (value - high.astype(F32)).astype(BF16)


def small_inverse(block):
    shape = (8, 8, 128)
    row, lane = 8 * iota(shape, 0) + iota(shape, 1), iota(shape, 2)
    work = jnp.where(lane < 64, block.reshape(shape), jnp.where(lane - 64 == row, 1.0, 0.0))
    for k in range(0, 64, 8):
        lines = [jnp.broadcast_to(work[k // 8, i : i + 1, :], (8, 128)) for i in range(8)]
        sides = [jnp.broadcast_to(work[:, :, k + j : k + j + 1], shape) for j in range(8)]
        corner = [[jnp.broadcast_to(sides[j][k // 8, i : i + 1, :], (8, 128)) for j in range(8)] for i in range(8)]
        update = jnp.zeros(shape, F32)
        for i in range(8):
            inverse = 1.0 / corner[i][i]
            update = update + jnp.where(row > k + i, sides[i], 0.0) * (lines[i] * inverse)
            for j in range(i + 1, 8):
                right = corner[i][j] * inverse
                below = corner[j][i] * inverse
                sides[j] = sides[j] - sides[i] * right
                lines[j] = lines[j] - below * lines[i]
                for m in range(i + 1, 8):
                    corner[j][m] = corner[j][m] - below * corner[i][m]
        work = work - update
    pivots = jnp.sum(jnp.where(lane == row, work, 0.0), axis=2, keepdims=True)
    return (work * lax.rsqrt(pivots)).reshape(64, 128)[:, 64:128]


def last_kernel(pieces, right, basis_out, block_out, gram, rest, inverse, sketch, value, result):
    for core in range(2):
        whole = pieces[core, 1152:1344, :].astype(F32) + pieces[core, 1344:1536, :].astype(F32)
        gram[128 * core : 128 * core + 128, 128 * core : 128 * core + 128] = whole[:128]
        gram[128 + 64 * core : 192 + 64 * core, :128] = whole[128:]
    gram[:128, 128:] = gram[128:, :128].T
    rest[...] = jnp.where(iota((256, 256), 0) == iota((256, 256), 1), 1.0, 0.0)
    inverse[...] = jnp.zeros((256, 256), F32)
    for step in range(4):
        top, tile = 64 * step, 128 * (step // 2)
        ahead, behind = (tile if step % 2 == 0 else 128), tile + 128
        block = gram[top : top + 64, tile : tile + 128]
        small = small_inverse(pltpu.roll(block, 64, 1) if step % 2 else block)
        lines = rest[top : top + 64, :behind]
        if step < 3:
            lines = jnp.concatenate([gram[top : top + 64, ahead:], lines], axis=1)
        lines = dot(small, lines, precision=HIGHEST)
        inverse[top : top + 64, :behind] = lines[:, lines.shape[1] - behind :]
        if step < 3:
            below = dot(lines[:, : 256 - ahead], lines, ((0,), (0,)), precision=HIGHEST)[top + 64 - ahead :]
            gram[top + 64 :, ahead:] = gram[top + 64 :, ahead:] - below[:, : 256 - ahead]
            rest[top + 64 :, :behind] = rest[top + 64 :, :behind] - below[:, 256 - ahead :]
    for core in range(2):
        for x in range(4):
            rows = pieces[core, 1536 + 24 * x : 1560 + 24 * x, :].astype(F32)
            sketch[18 * x : 18 * x + 18, 128 * core : 128 * core + 128] = rows[:18]
    high, low = split(inverse[...])
    own = sketch[...].astype(BF16)
    basis_out[...] = dot(own, high, ((1,), (1,))) + dot(own, low, ((1,), (1,)))
    for part in range(2):
        for core in range(2):
            lanes = slice(128 * core, 128 * core + 128)
            for tp in range(3):
                for t in range(3):
                    line = 576 * part + 64 * (3 * tp + t)
                    value[part, t, 64 * tp : 64 * tp + 64, lanes] = pieces[core, line : line + 64, :]
    wide = right[...].reshape(192, 512)
    for t in range(3):
        mixed = dot(high, value[0, t], ((1,), (1,))) + dot(low, value[0, t], ((1,), (1,)))
        mixed = mixed + dot(high, value[1, t], ((1,), (1,)))
        first, second = split(mixed)
        result[:, 512 * t : 512 * t + 512] = dot(first, wide) + dot(second, wide)
    upper = iota((8, 768), 0) < 4
    for pair in range(ROWS // 2):
        first = result[8 * pair : 8 * pair + 8, :768]
        second = result[8 * pair : 8 * pair + 8, 768:]
        block_out[2 * pair] = jnp.where(upper, first, pltpu.roll(second, 4, 0)).astype(BF16)
        block_out[2 * pair + 1] = jnp.where(upper, pltpu.roll(first, 4, 0), second).astype(BF16)


def block_kernel(pieces, out):
    total = jnp.sum(pieces[...].astype(F32), axis=0)
    picks = [stride_three(t, False) for t in range(3)]
    for j in range(4):
        lines = jnp.zeros((4, 384), F32)
        for t in range(3):
            start = 512 * t + 128 * j
            half, start = start // 768, start % 768
            rest = total[:, start : start + 128]
            spread = jnp.zeros((8, 384), F32)
            for _ in range(3):
                part = rest.astype(BF16)
                spread = spread + dot(part, picks[t])
                rest = rest - part.astype(F32)
            lines = lines + spread[4 * half : 4 * half + 4]
        out[:, 384 * j : 384 * j + 384] = lines


SMEM = pl.BlockSpec(memory_space=pltpu.SMEM)
VMEM = pl.BlockSpec(memory_space=pltpu.VMEM)
INTERPRET = False


def call(kernel, out, *args, smem=0, scratch=()):
    return pl.pallas_call(
        kernel,
        out_shape=[jax.ShapeDtypeStruct(*o) for o in out],
        in_specs=[SMEM] * smem + [VMEM] * (len(args) - smem),
        out_specs=[VMEM] * len(out),
        scratch_shapes=[pltpu.VMEM(*s) for s in scratch],
        compiler_params=pltpu.CompilerParams(vmem_limit_bytes=48 * 1024 * 1024),
        interpret=INTERPRET,
    )(*args)


PAIRS = [[0, 1], [2, 3], [4, 5], [6, 7]]
LINES_OF_X = [[0, 2, 4, 6], [1, 3, 5, 7]]


def exchange(value, axis, groups=None):
    return lax.all_to_all(value, axis, 0, 0, axis_index_groups=groups)


def exchange_lines(value, lines):
    return exchange(value.reshape(ROWS, lines // 2, 2, 128), "row").reshape(ROWS * lines, 128)


def local(left_site, right_site, gate, probes_matrix):
    place = jnp.stack([lax.axis_index("row"), lax.axis_index("col")]).astype(jnp.int32)
    left = left_site.transpose(1, 0, 2)
    right = right_site.transpose(1, 0, 2)
    (left_out,) = call(left_kernel, [((ROWS * 10, 128), BF16)], place, left, smem=1, scratch=[((ROWS * 10, 128), F32)])
    left_in = exchange_lines(left_out, 10)
    (weight,) = call(
        first_kernel,
        [((2, 192, 384), F32)],
        gate, right, probes_matrix,
        smem=1,
        scratch=[((3, 192, 256), F32)],
    )
    weight, left_in = lax.optimization_barrier((weight, left_in))
    weight = exchange(weight, "col", PAIRS)
    (weight,) = call(weight_kernel, [((4, 192, 384), BF16)], weight)
    weight = exchange(weight, "col", LINES_OF_X)
    sketch, left_rows = call(
        sketch_kernel,
        [((ROWS * 18, 128), BF16), ((384, 384), BF16)],
        left_in, weight,
        scratch=[((ROWS * 10, 128), F32), ((384, 384), BF16), ((384, 384), BF16), ((ROWS * 18, 128), F32)],
    )
    sketch = exchange_lines(sketch, 18)
    own, sketch = call(
        total_kernel,
        [((24, 128), BF16), ((ROWS * 18, 128), BF16)],
        sketch,
        scratch=[((72, 128), F32), ((144, 128), F32)],
    )
    sketch = exchange_lines(sketch, 18)
    other = lax.ppermute(sketch, "col", [(q, q ^ 1) for q in range(COLS)])
    (value,) = call(
        projection_kernel,
        [((4, 984, 128), BF16)],
        place, gate, sketch, other, left_rows, own,
        smem=2,
        scratch=[((ROWS * 18, 128), F32), ((384, 384), BF16), ((192, 384), F32), ((2, 128, 128), F32)],
    )
    value = exchange(value, "col", LINES_OF_X)
    (value,) = call(middle_kernel, [((2, 1632, 128), BF16)], value)
    value = exchange(value, "col", PAIRS)
    basis, block = call(
        last_kernel,
        [((72, 256), F32), ((ROWS, 8, 768), BF16)],
        value, right,
        scratch=[
            ((256, 256), F32), ((256, 256), F32), ((256, 256), F32), ((72, 256), F32),
            ((2, 3, 192, 256), BF16), ((256, 1536), F32),
        ],
    )
    block = exchange(block, "row")
    (new_block,) = call(block_kernel, [((4, 1536), F32)], block)
    return basis, new_block


def solution(mesh):
    return jax.shard_map(
        local,
        mesh=mesh,
        in_specs=(P("row", None, None), P("row", None, "col"), P(), P("col", None)),
        out_specs=(P("row", None), P("row", "col")),
        check_vma=False,
    )
```

time: 432 us -> 161 us (0.37)
  the two profiles are of different devices: /device:TPU:2 before, /device:TPU:8 now
where the time goes in v1:
time: 161 us
  blocking collectives  108 us (67%)
  Pallas kernels  20.4 us (13%)
  starting transfers between devices  18.6 us (12%)
  waiting for transfers between devices  12.1 us (8%)
    all_to_all x7, blocking collectives, exchange(): return lax.all_to_all(value, axis, 0, 0, axis_index_groups=groups)  108 us
    pallas_call x9, Pallas kernels, call(): pl.pallas_call(kernel, out_shape=[jax.ShapeDtypeStruct(*o) for o in out],...  20.4 us
    all_to_all x1, starting transfers between devices, exchange(): return lax.all_to_all(value, axis, 0, 0, axis_index_groups=groups)  16.7 us
    all_to_all x1, waiting for transfers between devices, exchange(): return lax.all_to_all(value, axis, 0, 0, axis_index_groups=groups)  10.5 us
  transfers between devices with their start and end apart: 2, of which 2 were waited for; matrix products, arithmetic and copies ran while one was open for 0% of the time, Pallas kernels for 1%

profile of v1, /device:TPU:8, one launch (start us, length us, event | category | flops | bytes accessed | tf_op | source)
XLA Modules:
  0.0 160.6 jit_solution(9930610491775379299)
XLA Ops:
  0.6 0.0 copy-start
  0.6 0.1 pad_add_fusion.place
  0.7 1.1 copy-done.2
  1.8 1.6 shard_map.60
  3.4 16.7 %all-to-all-start = ((bf16[64,5,2,128]{3,2,1,0:T(2,128)(2,1)}), bf16[64,5,2,128]{3,2,1,0:T(2,128)(2,1)S(1)}, u32[]{:S(2)}, u32[]{:S(2)}) async-start(bf16[64,5,2,128]{3,2,1,0:T(2,128)(2,1)} %bitcast.4), calls=%async_computation | async-start | bytes 327680 | tf_op jit(solution)/shard_map/all_to_all | solution.py:277
  20.2 0.0 copy-done
  20.2 1.9 %shard_map.59 = f32[2,192,384]{2,1,0:T(8,128)S(1)} custom-call(f32[9,9]{1,0:T(8,128)S(1)} %copy-done.3, bf16[3,64,512]{2,1,0:T(8,128)(2,1)S(1)} %bitcast.13, bf16[1536,256]{1,0:T(8,128)(2,1)S(1)} %copy-done), custom_call_target="tpu_custom_call" | custom-call | tf_op jit(solution)/shard_map/pallas_call | solution.py:261
  22.1 10.5 %all-to-all-done = bf16[64,5,2,128]{3,2,1,0:T(2,128)(2,1)S(1)} async-done(((bf16[64,5,2,128]{3,2,1,0:T(2,128)(2,1)}), bf16[64,5,2,128]{3,2,1,0:T(2,128)(2,1)S(1)}, u32[]{:S(2)}, u32[]{:S(2)}) %all-to-all-start) | async-done | bytes 163872 | tf_op jit(solution)/shard_map/all_to_all | solution.py:277
  32.7 4.2 %all_to_all.40.pieces = f32[2,192,384]{2,1,0:T(8,128)S(1)} all-to-all(f32[2,192,384]{2,1,0:T(8,128)S(1)} %shard_map.59), channel_id=1, replica_groups={{0,1},{2,3},{4,5},{6,7},{8,9},{10,11},{12,13},{14,15},{16,17},{18,19},{..., dimensions={0} | all-to-all | bytes 1179648 | tf_op jit(solution)/shard_map/all_to_all | solution.py:277
  36.9 0.1 shard_map.61
  36.9 14.6 %all_to_all.41.weight = bf16[4,192,384]{2,1,0:T(8,128)(2,1)S(1)} all-to-all(bf16[4,192,384]{2,1,0:T(8,128)(2,1)S(1)} %shard_map.61), channel_id=1, replica_groups={{0,2,4,6},{1,3,5,7},{8,10,12,14},{9,11,13,15},{16,18,20,22},{17,19,21,2..., dimensions={0} | all-to-all | bytes 1179648 | tf_op jit(solution)/shard_map/all_to_all | solution.py:277
  51.5 0.9 shard_map.62
  52.4 19.0 %all_to_all.42 = bf16[64,9,2,128]{3,2,1,0:T(2,128)(2,1)S(1)} all-to-all(bf16[64,9,2,128]{3,2,1,0:T(2,128)(2,1)S(1)} %bitcast.17), channel_id=1, replica_groups=mesh['row'=64,'col'=8] {'row'}, dimensions={0} | all-to-all | bytes 589824 | tf_op jit(solution)/shard_map/all_to_all | solution.py:277
  71.3 0.1 shard_map.63
  71.4 18.7 %all_to_all.43 = bf16[64,9,2,128]{3,2,1,0:T(2,128)(2,1)S(1)} all-to-all(bf16[64,9,2,128]{3,2,1,0:T(2,128)(2,1)S(1)} %bitcast.18), channel_id=1, replica_groups=mesh['row'=64,'col'=8] {'row'}, dimensions={0} | all-to-all | bytes 589824 | tf_op jit(solution)/shard_map/all_to_all | solution.py:277
  90.1 1.9 %collective-permute-start = (bf16[1152,128]{1,0:T(8,128)(2,1)S(1)}, bf16[1152,128]{1,0:T(8,128)(2,1)S(1)}, u32[]{:S(2)}, u32[]{:S(2)}) collective-permute-start(bf16[1152,128]{1,0:T(8,128)(2,1)S(1)} %bitcast.10), channel_id=1, source_target_pairs={{0,1},{1,0},{2,3},{3,2},{4,5},{5,4},{6,7},{7,6},{8,9},{9,8},{10,11... | collective-permute-start | bytes 884744 | tf_op jit(solution)/shard_map/ppermute | solution.py:315
  92.0 1.5 collective-permute-done.other_in
  93.5 1.5 shard_map.64
  95.0 17.6 %all_to_all.44.pieces = bf16[4,984,128]{2,1,0:T(8,128)(2,1)S(1)} all-to-all(bf16[4,984,128]{2,1,0:T(8,128)(2,1)S(1)} %shard_map.64), channel_id=1, replica_groups={{0,2,4,6},{1,3,5,7},{8,10,12,14},{9,11,13,15},{16,18,20,22},{17,19,21,2..., dimensions={0} | all-to-all | bytes 2015232 | tf_op jit(solution)/shard_map/all_to_all | solution.py:277
  112.7 0.2 shard_map.65
  112.8 4.4 %all_to_all.45.pieces = bf16[2,1632,128]{2,1,0:T(8,128)(2,1)S(1)} all-to-all(bf16[2,1632,128]{2,1,0:T(8,128)(2,1)S(1)} %shard_map.65), channel_id=1, replica_groups={{0,1},{2,3},{4,5},{6,7},{8,9},{10,11},{12,13},{14,15},{16,17},{18,19},{..., dimensions={0} | all-to-all | bytes 1671168 | tf_op jit(solution)/shard_map/all_to_all | solution.py:277
  117.2 12.9 %shard_map.66 = (f32[72,256]{1,0:T(8,128)}, bf16[64,8,768]{2,1,0:T(8,128)(2,1)S(1)}) custom-call(bf16[2,1632,128]{2,1,0:T(8,128)(2,1)S(1)} %all_to_all.45.pieces, bf16[3,64,512]{2,1,0:T(8,128)(2,1)S(1)} %bitcast.14), custom_call_target="tpu_custom_call" | custom-call | tf_op jit(solution)/shard_map/pallas_call | solution.py:261
  130.1 29.1 %all_to_all.46.pieces = bf16[64,8,768]{2,1,0:T(8,128)(2,1)S(1)} all-to-all(bf16[64,8,768]{2,1,0:T(8,128)(2,1)S(1)} %get-tuple-element.17), channel_id=1, replica_groups=mesh['row'=64,'col'=8] {'row'}, dimensions={0} | all-to-all | bytes 1572864 | tf_op jit(solution)/shard_map/all_to_all | solution.py:277
  159.2 1.4 shard_map.67
  (5 shorter events, 0.0 us)
Async XLA Ops:
  0.6 19.5 %copy-start = (bf16[1536,256]{1,0:T(8,128)(2,1)S(1)}, bf16[1536,256]{1,0:T(8,128)(2,1)}, u32[]{:S(2)}) copy-start(bf16[1536,256]{1,0:T(8,128)(2,1)} %probes.1) | copy-start | bytes 2359300
  0.7 1.1 copy-start.2
  3.4 16.7 %copy-start.1 = (bf16[64,3,512]{2,0,1:T(8,128)(2,1)S(1)}, bf16[64,3,512]{2,0,1:T(8,128)(2,1)}, u32[]{:S(2)}) copy-start(bf16[64,3,512]{2,0,1:T(8,128)(2,1)} %param.5) | copy-start | bytes 589828
  3.4 16.7 %copy-start.3 = (f32[9,9]{1,0:T(8,128)S(1)}, f32[9,9]{1,0:T(8,128)}, u32[]{:S(2)}) copy-start(f32[9,9]{1,0:T(8,128)} %gate.3) | copy-start | bytes 976
  3.4 29.2 %all-to-all-start = ((bf16[64,5,2,128]{3,2,1,0:T(2,128)(2,1)}), bf16[64,5,2,128]{3,2,1,0:T(2,128)(2,1)S(1)}, u32[]{:S(2)}, u32[]{:S(2)}) async-start(bf16[64,5,2,128]{3,2,1,0:T(2,128)(2,1)} %bitcast.4), calls=%async_computation | async-start | bytes 327680 | tf_op jit(solution)/shard_map/all_to_all | solution.py:277
  90.1 3.5 %collective-permute-start = (bf16[1152,128]{1,0:T(8,128)(2,1)S(1)}, bf16[1152,128]{1,0:T(8,128)(2,1)S(1)}, u32[]{:S(2)}, u32[]{:S(2)}) collective-permute-start(bf16[1152,128]{1,0:T(8,128)(2,1)S(1)} %bitcast.10), channel_id=1, source_target_pairs={{0,1},{1,0},{2,3},{3,2},{4,5},{5,4},{6,7},{7,6},{8,9},{9,8},{10,11... | collective-permute-start | bytes 884744 | tf_op jit(solution)/shard_map/ppermute | solution.py:315

commit v2 on v1

--- a/solution.py
+++ b/solution.py
@@ -44,29 +44,24 @@
     left_out[...] = lines[...].astype(BF16)
 
 
-def first_kernel(gate, right, probes, weight_out, product):
-    wide = right[...].reshape(192, 512)
+def first_kernel(place, gate, right, probes, right_other, probes_other, weight_out, product):
+    half = pl.ds(pl.multiple_of(128 * (place[1] % 2), 128), 128)
     for t in range(3):
         pick = stride_three(t, False)
-        own = jnp.concatenate(
-            [dot(pick, probes[384 * j : 384 * j + 384, :]).astype(BF16) for j in range(4)], axis=0
-        )
-        product[t] = dot(wide, own)
+        total = jnp.zeros((192, 128), F32)
+        for side, probe in ((right, probes), (right_other, probes_other)):
+            own = [dot(pick, probe[384 * j : 384 * j + 384, half]).astype(BF16) for j in range(4)]
+            total = total + dot(side[...].reshape(192, 512), jnp.concatenate(own, axis=0))
+        product[t] = total
     for up in range(3):
         for s in range(3):
-            total = jnp.zeros((64, 256), F32)
+            total = jnp.zeros((64, 128), F32)
             for tp in range(3):
                 for t in range(3):
                     total = total + gate[3 * s + t, 3 * up + tp] * product[t, 64 * tp : 64 * tp + 64, :]
-            for core in range(2):
-                half = total[:, 128 * core : 128 * core + 128]
-                weight_out[core, 64 * up : 64 * up + 64, 128 * s : 128 * s + 128] = half
-
-
-def weight_kernel(pieces, out):
-    total = (pieces[0] + pieces[1]).astype(BF16)
-    for x in range(4):
-        out[x] = total
+            total = total.astype(BF16)
+            for x in range(4):
+                weight_out[x, 64 * up : 64 * up + 64, 128 * s : 128 * s + 128] = total
 
 
 def sketch_kernel(left_in, weight, sketch_out, left_rows, wide_left, high, low, wide_sketch):
@@ -106,8 +101,7 @@
         out[144 * k : 144 * k + 144, :] = total
 
 
-def projection_kernel(place, gate, sketch_in, other_in, left_rows, own, out, wide_sketch, sketch, product, cross):
-    core = place[1] % 2
+def value_kernel(gate, sketch_in, left_rows, out, wide_sketch, sketch, product):
     wide_sketch[...] = sketch_in[...].astype(F32)
     for i in range(6):
         for s in range(3):
@@ -124,20 +118,22 @@
                     part = product[64 * up : 64 * up + 64, 128 * s : 128 * s + 128]
                     total = total + gate[3 * s + t, 3 * up + tp] * part
             line = 64 * (3 * tp + t)
-            total = total.astype(BF16)
-            for x in range(4):
-                out[x, line : line + 64, :] = total
+            out[line : line + 64, :] = total.astype(BF16)
+
+
+def gram_kernel(place, sketch_in, other_in, value, own, out, cross):
+    core = place[1] % 2
     mine, other = sketch_in[...], other_in[...]
     block = dot(mine, mine, ((0,), (0,)))
     cross[0] = dot(other, mine, ((0,), (0,)))
     cross[1] = dot(mine, other, ((0,), (0,)))
     half = cross[core, pl.ds(pl.multiple_of(64 * core, 64), 64), :]
-    for start, part in ((0, block), (128, half)):
-        size = part.shape[0]
-        for line, piece in zip((576 + start, 768 + start), split(part)):
-            for x in range(4):
-                out[x, line : line + size, :] = piece
+    block, half = split(block), split(half)
     for x in range(4):
+        out[x, :576, :] = value[...]
+        for part in range(2):
+            out[x, 576 + 192 * part : 704 + 192 * part, :] = block[part]
+            out[x, 704 + 192 * part : 768 + 192 * part, :] = half[part]
         out[x, 960:984, :] = own[...]
 
 
@@ -281,22 +277,26 @@
     return exchange(value.reshape(ROWS, lines // 2, 2, 128), "row").reshape(ROWS * lines, 128)
 
 
+def swap(value):
+    return lax.ppermute(value, "col", [(q, q ^ 1) for q in range(COLS)])
+
+
 def local(left_site, right_site, gate, probes_matrix):
     place = jnp.stack([lax.axis_index("row"), lax.axis_index("col")]).astype(jnp.int32)
     left = left_site.transpose(1, 0, 2)
     right = right_site.transpose(1, 0, 2)
     (left_out,) = call(left_kernel, [((ROWS * 10, 128), BF16)], place, left, smem=1, scratch=[((ROWS * 10, 128), F32)])
     left_in = exchange_lines(left_out, 10)
+    right_other = swap(right)
+    probes_other = swap(probes_matrix)
     (weight,) = call(
         first_kernel,
-        [((2, 192, 384), F32)],
-        gate, right, probes_matrix,
-        smem=1,
-        scratch=[((3, 192, 256), F32)],
+        [((4, 192, 384), BF16)],
+        place, gate, right, probes_matrix, right_other, probes_other,
+        smem=2,
+        scratch=[((3, 192, 128), F32)],
     )
     weight, left_in = lax.optimization_barrier((weight, left_in))
-    weight = exchange(weight, "col", PAIRS)
-    (weight,) = call(weight_kernel, [((4, 192, 384), BF16)], weight)
     weight = exchange(weight, "col", LINES_OF_X)
     sketch, left_rows = call(
         sketch_kernel,
@@ -312,13 +312,20 @@
         scratch=[((72, 128), F32), ((144, 128), F32)],
     )
     sketch = exchange_lines(sketch, 18)
-    other = lax.ppermute(sketch, "col", [(q, q ^ 1) for q in range(COLS)])
+    other = swap(sketch)
     (value,) = call(
-        projection_kernel,
+        value_kernel,
+        [((576, 128), BF16)],
+        gate, sketch, left_rows,
+        smem=1,
+        scratch=[((ROWS * 18, 128), F32), ((384, 384), BF16), ((192, 384), F32)],
+    )
+    (value,) = call(
+        gram_kernel,
         [((4, 984, 128), BF16)],
-        place, gate, sketch, other, left_rows, own,
-        smem=2,
-        scratch=[((ROWS * 18, 128), F32), ((384, 384), BF16), ((192, 384), F32), ((2, 128, 128), F32)],
+        place, sketch, other, value, own,
+        smem=1,
+        scratch=[((2, 128, 128), F32)],
     )
     value = exchange(value, "col", LINES_OF_X)
     (value,) = call(middle_kernel, [((2, 1632, 128), BF16)], value)

time: 161 us -> 160 us (level)
  blocking collectives: 108 us -> 104 us
  starting transfers between devices: 18.6 us -> 22.6 us
  waiting for transfers between devices: 12.1 us -> 9.29 us
    ppermute x1 -> x3, starting transfers between devices: 1.91 us -> 5.88 us  [swap(): return lax.ppermute(value, 'col', [(q, q ^ 1) for q in range(COLS)])]
    all_to_all x7 -> x6, blocking collectives: 108 us -> 104 us  [exchange(): return lax.all_to_all(value, axis, 0, 0, axis_index_groups=groups)]
    all_to_all x1, waiting for transfers between devices: 10.5 us -> 7.52 us  [exchange(): return lax.all_to_all(value, axis, 0, 0, axis_index_groups=groups)]
  transfers between devices with their start and end apart: 2 -> 4, of which waited for: 2 -> 3; matrix products, arithmetic and copies ran while one was open for 0% -> 0% of each run, Pallas kernels for 1% -> 3%
where the time goes in v2:
time: 160 us; the launch traced here: 159 us
  blocking collectives  104 us (65%)
  starting transfers between devices  22.6 us (14%)
  Pallas kernels  21.4 us (13%)
  waiting for transfers between devices  9.29 us (6%)
    all_to_all x6, blocking collectives, exchange(): return lax.all_to_all(value, axis, 0, 0, axis_index_groups=groups)  104 us
    pallas_call x9, Pallas kernels, call(): pl.pallas_call(kernel, out_shape=[jax.ShapeDtypeStruct(*o) for o in out],...  21.4 us
    all_to_all x1, starting transfers between devices, exchange(): return lax.all_to_all(value, axis, 0, 0, axis_index_groups=groups)  16.7 us
    all_to_all x1, waiting for transfers between devices, exchange(): return lax.all_to_all(value, axis, 0, 0, axis_index_groups=groups)  7.52 us
    ppermute x3, starting transfers between devices, swap(): return lax.ppermute(value, 'col', [(q, q ^ 1) for q in range(COLS)])  5.88 us
  transfers between devices with their start and end apart: 4, of which 3 were waited for; matrix products, arithmetic and copies ran while one was open for 0% of the time, Pallas kernels for 3%

profile of v2, /device:TPU:8, one launch (start us, length us, event | category | flops | bytes accessed | tf_op | source)
XLA Modules:
  0.0 159.2 jit_solution(9940502768879755597)
XLA Ops:
  0.6 2.1 %collective-permute-start.1 = (bf16[1536,256]{1,0:T(8,128)(2,1)}, bf16[1536,256]{1,0:T(8,128)(2,1)S(1)}, u32[]{:S(2)}, u32[]{:S(2)}) collective-permute-start(bf16[1536,256]{1,0:T(8,128)(2,1)} %probes.1), channel_id=1, source_target_pairs={{0,1},{1,0},{2,3},{3,2},{4,5},{5,4},{6,7},{7,6},{8,9},{9,8},{10,11... | collective-permute-start | bytes 2359304 | tf_op jit(solution)/shard_map/ppermute | solution.py:281
  2.7 0.1 pad_add_fusion.place
  2.8 1.1 copy-done.2
  3.8 1.6 %shard_map.60 = bf16[640,128]{1,0:T(8,128)(2,1)} custom-call(s32[2]{0:T(128)S(1)} %pad_add_fusion.place, bf16[3,24,4096]{2,1,0:T(8,128)(2,1)S(1)} %bitcast.18), custom_call_target="tpu_custom_call" | custom-call | tf_op jit(solution)/shard_map/pallas_call | solution.py:257
  5.5 16.7 %all-to-all-start = ((bf16[64,5,2,128]{3,2,1,0:T(2,128)(2,1)}), bf16[64,5,2,128]{3,2,1,0:T(2,128)(2,1)S(1)}, u32[]{:S(2)}, u32[]{:S(2)}) async-start(bf16[64,5,2,128]{3,2,1,0:T(2,128)(2,1)} %bitcast.4), calls=%async_computation | async-start | bytes 327680 | tf_op jit(solution)/shard_map/all_to_all | solution.py:273
  22.2 1.9 %collective-permute-start = (bf16[3,64,512]{2,1,0:T(8,128)(2,1)S(1)}, bf16[3,64,512]{2,1,0:T(8,128)(2,1)S(1)}, u32[]{:S(2)}, u32[]{:S(2)}) collective-permute-start(bf16[3,64,512]{2,1,0:T(8,128)(2,1)S(1)} %bitcast.14), channel_id=1, source_target_pairs={{0,1},{1,0},{2,3},{3,2},{4,5},{5,4},{6,7},{7,6},{8,9},{9,8},{10,11... | collective-permute-start | bytes 589832 | tf_op jit(solution)/shard_map/ppermute | solution.py:281
  24.1 1.4 collective-permute-done.right_other
  25.5 2.3 %shard_map.59 = bf16[4,192,384]{2,1,0:T(8,128)(2,1)S(1)} custom-call(s32[2]{0:T(128)S(1)} %pad_add_fusion.place, f32[9,9]{1,0:T(8,128)S(1)} %copy-done.3, bf16[3,64,512]{2,1,0:T(8,128)(2,1)S(1)} %bitcast.15, bf16[1536,256]{1,0:T(8,128)(2,1)S(1)} %copy-done, bf16[3,64,512]{2,1,0:T(8,128)(2,1)S(1)} %collective-permute-done.right_other, ...), custom_call_target="tpu_custom_call" | custom-call | tf_op jit(solution)/shard_map/pallas_call | solution.py:257
  27.8 7.5 %all-to-all-done = bf16[64,5,2,128]{3,2,1,0:T(2,128)(2,1)S(1)} async-done(((bf16[64,5,2,128]{3,2,1,0:T(2,128)(2,1)}), bf16[64,5,2,128]{3,2,1,0:T(2,128)(2,1)S(1)}, u32[]{:S(2)}, u32[]{:S(2)}) %all-to-all-start) | async-done | bytes 163872 | tf_op jit(solution)/shard_map/all_to_all | solution.py:273
  35.3 13.3 %all_to_all.35.weight = bf16[4,192,384]{2,1,0:T(8,128)(2,1)S(1)} all-to-all(bf16[4,192,384]{2,1,0:T(8,128)(2,1)S(1)} %shard_map.59), channel_id=1, replica_groups={{0,2,4,6},{1,3,5,7},{8,10,12,14},{9,11,13,15},{16,18,20,22},{17,19,21,2..., dimensions={0} | all-to-all | bytes 1179648 | tf_op jit(solution)/shard_map/all_to_all | solution.py:273
  48.6 0.9 shard_map.61
  49.5 20.4 %all_to_all.36 = bf16[64,9,2,128]{3,2,1,0:T(2,128)(2,1)S(1)} all-to-all(bf16[64,9,2,128]{3,2,1,0:T(2,128)(2,1)S(1)} %bitcast.19), channel_id=1, replica_groups=mesh['row'=64,'col'=8] {'row'}, dimensions={0} | all-to-all | bytes 589824 | tf_op jit(solution)/shard_map/all_to_all | solution.py:273
  69.9 0.1 shard_map.62
  70.0 19.2 %all_to_all.37 = bf16[64,9,2,128]{3,2,1,0:T(2,128)(2,1)S(1)} all-to-all(bf16[64,9,2,128]{3,2,1,0:T(2,128)(2,1)S(1)} %bitcast.20), channel_id=1, replica_groups=mesh['row'=64,'col'=8] {'row'}, dimensions={0} | all-to-all | bytes 589824 | tf_op jit(solution)/shard_map/all_to_all | solution.py:273
  89.2 1.9 %collective-permute-start.2 = (bf16[1152,128]{1,0:T(8,128)(2,1)S(1)}, bf16[1152,128]{1,0:T(8,128)(2,1)S(1)}, u32[]{:S(2)}, u32[]{:S(2)}) collective-permute-start(bf16[1152,128]{1,0:T(8,128)(2,1)S(1)} %bitcast.10), channel_id=1, source_target_pairs={{0,1},{1,0},{2,3},{3,2},{4,5},{5,4},{6,7},{7,6},{8,9},{9,8},{10,11... | collective-permute-start | bytes 884744 | tf_op jit(solution)/shard_map/ppermute | solution.py:281
  91.1 1.2 shard_map.63.value
  92.3 0.4 collective-permute-done.2.other_in
  92.6 1.0 shard_map.64
  93.6 17.7 %all_to_all.38.pieces = bf16[4,984,128]{2,1,0:T(8,128)(2,1)S(1)} all-to-all(bf16[4,984,128]{2,1,0:T(8,128)(2,1)S(1)} %shard_map.64), channel_id=1, replica_groups={{0,2,4,6},{1,3,5,7},{8,10,12,14},{9,11,13,15},{16,18,20,22},{17,19,21,2..., dimensions={0} | all-to-all | bytes 2015232 | tf_op jit(solution)/shard_map/all_to_all | solution.py:273
  111.3 0.2 shard_map.65
  111.5 4.4 %all_to_all.39.pieces = bf16[2,1632,128]{2,1,0:T(8,128)(2,1)S(1)} all-to-all(bf16[2,1632,128]{2,1,0:T(8,128)(2,1)S(1)} %shard_map.65), channel_id=1, replica_groups={{0,1},{2,3},{4,5},{6,7},{8,9},{10,11},{12,13},{14,15},{16,17},{18,19},{..., dimensions={0} | all-to-all | bytes 1671168 | tf_op jit(solution)/shard_map/all_to_all | solution.py:273
  115.9 12.9 %shard_map.66 = (f32[72,256]{1,0:T(8,128)}, bf16[64,8,768]{2,1,0:T(8,128)(2,1)S(1)}) custom-call(bf16[2,1632,128]{2,1,0:T(8,128)(2,1)S(1)} %all_to_all.39.pieces, bf16[3,64,512]{2,1,0:T(8,128)(2,1)S(1)} %bitcast.16), custom_call_target="tpu_custom_call" | custom-call | tf_op jit(solution)/shard_map/pallas_call | solution.py:257
  128.7 29.0 %all_to_all.40.pieces = bf16[64,8,768]{2,1,0:T(8,128)(2,1)S(1)} all-to-all(bf16[64,8,768]{2,1,0:T(8,128)(2,1)S(1)} %get-tuple-element.17), channel_id=1, replica_groups=mesh['row'=64,'col'=8] {'row'}, dimensions={0} | all-to-all | bytes 1572864 | tf_op jit(solution)/shard_map/all_to_all | solution.py:273
  157.8 1.4 shard_map.67
  (8 shorter events, 0.0 us)
Async XLA Ops:
  0.6 24.9 %copy-start = (bf16[1536,256]{1,0:T(8,128)(2,1)S(1)}, bf16[1536,256]{1,0:T(8,128)(2,1)}, u32[]{:S(2)}) copy-start(bf16[1536,256]{1,0:T(8,128)(2,1)} %probes.1) | copy-start | bytes 2359300
  0.6 24.9 %collective-permute-start.1 = (bf16[1536,256]{1,0:T(8,128)(2,1)}, bf16[1536,256]{1,0:T(8,128)(2,1)S(1)}, u32[]{:S(2)}, u32[]{:S(2)}) collective-permute-start(bf16[1536,256]{1,0:T(8,128)(2,1)} %probes.1), channel_id=1, source_target_pairs={{0,1},{1,0},{2,3},{3,2},{4,5},{5,4},{6,7},{7,6},{8,9},{9,8},{10,11... | collective-permute-start | bytes 2359304 | tf_op jit(solution)/shard_map/ppermute | solution.py:281
  2.8 1.1 copy-start.2
  5.5 16.7 %copy-start.1 = (bf16[64,3,512]{2,0,1:T(8,128)(2,1)S(1)}, bf16[64,3,512]{2,0,1:T(8,128)(2,1)}, u32[]{:S(2)}) copy-start(bf16[64,3,512]{2,0,1:T(8,128)(2,1)} %param.5) | copy-start | bytes 589828
  5.5 20.1 %copy-start.3 = (f32[9,9]{1,0:T(8,128)S(1)}, f32[9,9]{1,0:T(8,128)}, u32[]{:S(2)}) copy-start(f32[9,9]{1,0:T(8,128)} %gate.3) | copy-start | bytes 976
  5.5 29.9 %all-to-all-start = ((bf16[64,5,2,128]{3,2,1,0:T(2,128)(2,1)}), bf16[64,5,2,128]{3,2,1,0:T(2,128)(2,1)S(1)}, u32[]{:S(2)}, u32[]{:S(2)}) async-start(bf16[64,5,2,128]{3,2,1,0:T(2,128)(2,1)} %bitcast.4), calls=%async_computation | async-start | bytes 327680 | tf_op jit(solution)/shard_map/all_to_all | solution.py:273
  22.2 3.3 %collective-permute-start = (bf16[3,64,512]{2,1,0:T(8,128)(2,1)S(1)}, bf16[3,64,512]{2,1,0:T(8,128)(2,1)S(1)}, u32[]{:S(2)}, u32[]{:S(2)}) collective-permute-start(bf16[3,64,512]{2,1,0:T(8,128)(2,1)S(1)} %bitcast.14), channel_id=1, source_target_pairs={{0,1},{1,0},{2,3},{3,2},{4,5},{5,4},{6,7},{7,6},{8,9},{9,8},{10,11... | collective-permute-start | bytes 589832 | tf_op jit(solution)/shard_map/ppermute | solution.py:281
  89.2 3.5 %collective-permute-start.2 = (bf16[1152,128]{1,0:T(8,128)(2,1)S(1)}, bf16[1152,128]{1,0:T(8,128)(2,1)S(1)}, u32[]{:S(2)}, u32[]{:S(2)}) collective-permute-start(bf16[1152,128]{1,0:T(8,128)(2,1)S(1)} %bitcast.10), channel_id=1, source_target_pairs={{0,1},{1,0},{2,3},{3,2},{4,5},{5,4},{6,7},{7,6},{8,9},{9,8},{10,11... | collective-permute-start | bytes 884744 | tf_op jit(solution)/shard_map/ppermute | solution.py:281

commit v3 on v2

--- a/solution.py
+++ b/solution.py
@@ -27,20 +27,36 @@
     return jnp.where(column == 3 * b + t, 1.0, 0.0).astype(BF16)
 
 
-def left_kernel(place, left, left_out, lines):
-    row, column, lane = iota((16, 72), 0), iota((16, 72), 1), iota((16, 128), 1)
-    sides = []
+def left_kernel(place, left, left_out, rows, lines, arrived):
+    x = place[1] // 2
+    start = pl.multiple_of(8 * (x // 2), 8)
+    copies = [
+        pltpu.make_async_copy(
+            left.at[:, pl.ds(start, 16), 1024 * part : 1024 * part + 1024],
+            rows.at[part],
+            arrived.at[part],
+        )
+        for part in range(4)
+    ]
+    for copy in copies:
+        copy.start()
+    row, column, lane = iota((16, 48), 0), iota((16, 48), 1), iota((16, 128), 1)
+    picks = []
     for h in range(2):
         line = 2 * row + h
         photon = jnp.where(line < 6, 0, jnp.where(line < 12, 1, 2))
-        chosen = (column == photon * 24 + 6 * (place[1] // 2) + line - 6 * photon) & (line < 18)
-        sides.append(dot(jnp.where(chosen, 1.0, 0.0).astype(BF16), left[...].reshape(72, 4096)))
-    for pair in range(ROWS // 2):
-        even, odd = (side[:, 128 * pair : 128 * pair + 128] for side in sides)
-        first = jnp.where(lane < 64, even, pltpu.roll(odd, 64, 1))
-        second = jnp.where(lane < 64, pltpu.roll(even, 64, 1), odd)
-        lines[20 * pair : 20 * pair + 10, :] = first[:10]
-        lines[20 * pair + 10 : 20 * pair + 20, :] = second[:10]
+        chosen = (column == photon * 16 + 6 * x - start + line - 6 * photon) & (line < 18)
+        picks.append(jnp.where(chosen, 1.0, 0.0).astype(BF16))
+    for part in range(4):
+        copies[part].wait()
+        sides = [dot(pick, rows[part].reshape(48, 1024)) for pick in picks]
+        for pair in range(8):
+            even, odd = (side[:, 128 * pair : 128 * pair + 128] for side in sides)
+            first = jnp.where(lane < 64, even, pltpu.roll(odd, 64, 1))
+            second = jnp.where(lane < 64, pltpu.roll(even, 64, 1), odd)
+            at = 160 * part + 20 * pair
+            lines[at : at + 10, :] = first[:10]
+            lines[at + 10 : at + 20, :] = second[:10]
     left_out[...] = lines[...].astype(BF16)
 
 
@@ -142,13 +158,12 @@
         pieces[2, :960].astype(F32) + pieces[3, :960].astype(F32)
     )
     value, gram = split(total[:576]), split(total[576:768] + total[768:960])
-    for core in range(2):
-        out[core, :576, :] = value[0]
-        out[core, 576:1152, :] = value[1]
-        out[core, 1152:1344, :] = gram[0]
-        out[core, 1344:1536, :] = gram[1]
-        for x in range(4):
-            out[core, 1536 + 24 * x : 1560 + 24 * x, :] = pieces[x, 960:984, :]
+    out[:576, :] = value[0]
+    out[576:1152, :] = value[1]
+    out[1152:1344, :] = gram[0]
+    out[1344:1536, :] = gram[1]
+    for x in range(4):
+        out[1536 + 24 * x : 1560 + 24 * x, :] = pieces[x, 960:984, :]
 
 
 def split(value):
@@ -157,34 +172,58 @@
 
 
 def small_inverse(block):
-    shape = (8, 8, 128)
-    row, lane = 8 * iota(shape, 0) + iota(shape, 1), iota(shape, 2)
-    work = jnp.where(lane < 64, block.reshape(shape), jnp.where(lane - 64 == row, 1.0, 0.0))
+    row, lane, sub = iota((64, 128), 0), iota((64, 128), 1), iota((8, 128), 0)
+    diagonal = jnp.where(lane == row, block, 0.0)
+    tall = lax.rsqrt(jnp.sum(diagonal, axis=1, keepdims=True))
+    flat = jnp.sum(diagonal, axis=0, keepdims=True)
+    flat = lax.rsqrt(jnp.where(iota((1, 128), 1) < 64, flat, 1.0))
+    tail = jnp.where(lane < 64, block * tall * flat, jnp.where(lane - 64 == row, 1.0, 0.0)).reshape(8, 8, 128)
+    done = []
     for k in range(0, 64, 8):
-        lines = [jnp.broadcast_to(work[k // 8, i : i + 1, :], (8, 128)) for i in range(8)]
-        sides = [jnp.broadcast_to(work[:, :, k + j : k + j + 1], shape) for j in range(8)]
-        corner = [[jnp.broadcast_to(sides[j][k // 8, i : i + 1, :], (8, 128)) for j in range(8)] for i in range(8)]
-        update = jnp.zeros(shape, F32)
-        for i in range(8):
-            inverse = 1.0 / corner[i][i]
-            update = update + jnp.where(row > k + i, sides[i], 0.0) * (lines[i] * inverse)
-            for j in range(i + 1, 8):
-                right = corner[i][j] * inverse
-                below = corner[j][i] * inverse
-                sides[j] = sides[j] - sides[i] * right
-                lines[j] = lines[j] - below * lines[i]
-                for m in range(i + 1, 8):
-                    corner[j][m] = corner[j][m] - below * corner[i][m]
-        work = work - update
-    pivots = jnp.sum(jnp.where(lane == row, work, 0.0), axis=2, keepdims=True)
-    return (work * lax.rsqrt(pivots)).reshape(64, 128)[:, 64:128]
-
-
-def last_kernel(pieces, right, basis_out, block_out, gram, rest, inverse, sketch, value, result):
-    for core in range(2):
-        whole = pieces[core, 1152:1344, :].astype(F32) + pieces[core, 1344:1536, :].astype(F32)
-        gram[128 * core : 128 * core + 128, 128 * core : 128 * core + 128] = whole[:128]
-        gram[128 + 64 * core : 192 + 64 * core, :128] = whole[128:]
+        head, tail = tail[0], tail[1:]
+        count = tail.shape[0]
+        lines = [jnp.broadcast_to(head[i : i + 1, :], (8, 128)) for i in range(8)]
+        corner = [
+            [jnp.broadcast_to(lines[i][:, k + j : k + j + 1], (8, 128)) if j >= i else None for j in range(8)]
+            for i in range(8)
+        ]
+        if count:
+            sides = [jnp.broadcast_to(tail[:, :, k + j : k + j + 1], tail.shape) for j in range(8)]
+        for i in range(0, 8, 2):
+            first, both, second = corner[i][i], corner[i][i + 1], corner[i + 1][i + 1]
+            inverse = 1.0 / first
+            ratio = both * inverse
+            inverse_two = first * (1.0 / (first * second - both * both))
+            lines[i + 1] = lines[i + 1] - ratio * lines[i]
+            above, below = lines[i] * inverse, lines[i + 1] * inverse_two
+            upper = corner[i]
+            lower = [None if m <= i + 1 else corner[i + 1][m] - ratio * upper[m] for m in range(8)]
+            if count:
+                sides[i + 1] = sides[i + 1] - ratio * sides[i]
+                tail = tail - (sides[i] * above + sides[i + 1] * below)
+            for j in range(i + 2, 8):
+                one, two = upper[j] * inverse, lower[j] * inverse_two
+                lines[j] = lines[j] - (one * lines[i] + two * lines[i + 1])
+                if count:
+                    sides[j] = sides[j] - (one * sides[i] + two * sides[i + 1])
+                for m in range(j, 8):
+                    corner[j][m] = corner[j][m] - (one * upper[m] + two * lower[m])
+        head = lines[7]
+        for i in range(7):
+            head = jnp.where(sub == i, lines[i], head)
+        done.append(head)
+    work = jnp.concatenate(done, axis=0)
+    pivots = jnp.sum(jnp.where(lane == row, work, 0.0), axis=1, keepdims=True)
+    return (work * lax.rsqrt(pivots))[:, 64:128] * flat[:, :64]
+
+
+def last_kernel(place, mine, other, right, basis_out, block_out, gram, rest, inverse, sketch, value, result):
+    core = place[1] % 2
+    halves = [(side, pl.ds(pl.multiple_of(128 * k, 128), 128), k) for side, k in ((mine, core), (other, 1 - core))]
+    for pieces, half, k in halves:
+        whole = pieces[1152:1344, :].astype(F32) + pieces[1344:1536, :].astype(F32)
+        gram[half, half] = whole[:128]
+        gram[pl.ds(pl.multiple_of(128 + 64 * k, 64), 64), :128] = whole[128:]
     gram[:128, 128:] = gram[128:, :128].T
     rest[...] = jnp.where(iota((256, 256), 0) == iota((256, 256), 1), 1.0, 0.0)
     inverse[...] = jnp.zeros((256, 256), F32)
@@ -202,20 +241,19 @@
             below = dot(lines[:, : 256 - ahead], lines, ((0,), (0,)), precision=HIGHEST)[top + 64 - ahead :]
             gram[top + 64 :, ahead:] = gram[top + 64 :, ahead:] - below[:, : 256 - ahead]
             rest[top + 64 :, :behind] = rest[top + 64 :, :behind] - below[:, 256 - ahead :]
-    for core in range(2):
+    for pieces, half, _ in halves:
         for x in range(4):
-            rows = pieces[core, 1536 + 24 * x : 1560 + 24 * x, :].astype(F32)
-            sketch[18 * x : 18 * x + 18, 128 * core : 128 * core + 128] = rows[:18]
+            rows = pieces[1536 + 24 * x : 1560 + 24 * x, :].astype(F32)
+            sketch[18 * x : 18 * x + 18, half] = rows[:18]
     high, low = split(inverse[...])
     own = sketch[...].astype(BF16)
     basis_out[...] = dot(own, high, ((1,), (1,))) + dot(own, low, ((1,), (1,)))
     for part in range(2):
-        for core in range(2):
-            lanes = slice(128 * core, 128 * core + 128)
+        for pieces, half, _ in halves:
             for tp in range(3):
                 for t in range(3):
                     line = 576 * part + 64 * (3 * tp + t)
-                    value[part, t, 64 * tp : 64 * tp + 64, lanes] = pieces[core, line : line + 64, :]
+                    value[part, t, 64 * tp : 64 * tp + 64, half] = pieces[line : line + 64, :]
     wide = right[...].reshape(192, 512)
     for t in range(3):
         mixed = dot(high, value[0, t], ((1,), (1,))) + dot(low, value[0, t], ((1,), (1,)))
@@ -253,19 +291,20 @@
 INTERPRET = False
 
 
-def call(kernel, out, *args, smem=0, scratch=()):
+def call(kernel, out, *args, smem=0, far=0, scratch=(), copies=0):
+    near = len(args) - smem - far
+    shapes = [pltpu.VMEM(*s) for s in scratch]
     return pl.pallas_call(
         kernel,
         out_shape=[jax.ShapeDtypeStruct(*o) for o in out],
-        in_specs=[SMEM] * smem + [VMEM] * (len(args) - smem),
+        in_specs=[SMEM] * smem + [VMEM] * near + [pl.BlockSpec(memory_space=pltpu.HBM)] * far,
         out_specs=[VMEM] * len(out),
-        scratch_shapes=[pltpu.VMEM(*s) for s in scratch],
+        scratch_shapes=shapes + ([pltpu.SemaphoreType.DMA((copies,))] if copies else []),
         compiler_params=pltpu.CompilerParams(vmem_limit_bytes=48 * 1024 * 1024),
         interpret=INTERPRET,
     )(*args)
 
 
-PAIRS = [[0, 1], [2, 3], [4, 5], [6, 7]]
 LINES_OF_X = [[0, 2, 4, 6], [1, 3, 5, 7]]
 
 
@@ -285,7 +324,15 @@
     place = jnp.stack([lax.axis_index("row"), lax.axis_index("col")]).astype(jnp.int32)
     left = left_site.transpose(1, 0, 2)
     right = right_site.transpose(1, 0, 2)
-    (left_out,) = call(left_kernel, [((ROWS * 10, 128), BF16)], place, left, smem=1, scratch=[((ROWS * 10, 128), F32)])
+    (left_out,) = call(
+        left_kernel,
+        [((ROWS * 10, 128), BF16)],
+        place, pltpu.with_memory_space_constraint(left, pltpu.HBM),
+        smem=1,
+        far=1,
+        scratch=[((4, 3, 16, 1024), BF16), ((ROWS * 10, 128), F32)],
+        copies=4,
+    )
     left_in = exchange_lines(left_out, 10)
     right_other = swap(right)
     probes_other = swap(probes_matrix)
@@ -328,12 +375,12 @@
         scratch=[((2, 128, 128), F32)],
     )
     value = exchange(value, "col", LINES_OF_X)
-    (value,) = call(middle_kernel, [((2, 1632, 128), BF16)], value)
-    value = exchange(value, "col", PAIRS)
+    (value,) = call(middle_kernel, [((1632, 128), BF16)], value)
     basis, block = call(
         last_kernel,
         [((72, 256), F32), ((ROWS, 8, 768), BF16)],
-        value, right,
+        place, value, swap(value), right,
+        smem=1,
         scratch=[
             ((256, 256), F32), ((256, 256), F32), ((256, 256), F32), ((72, 256), F32),
             ((2, 3, 192, 256), BF16), ((256, 1536), F32),

time: 160 us -> 159 us (level)
  blocking collectives: 104 us -> 99.5 us
  starting transfers between devices: 22.6 us -> 24.7 us
  Pallas kernels: 21.4 us -> 23 us
    all_to_all x6 -> x5, blocking collectives: 104 us -> 99.5 us  [exchange(): return lax.all_to_all(value, axis, 0, 0, axis_index_groups=groups)]
    ppermute x3 -> x4, starting transfers between devices: 5.88 us -> 7.98 us  [swap(): return lax.ppermute(value, 'col', [(q, q ^ 1) for q in range(COLS)])]
    ppermute x3 -> x4, waiting for transfers between devices: 1.77 us -> 3.31 us  [swap(): return lax.ppermute(value, 'col', [(q, q ^ 1) for q in range(COLS)])]
  transfers between devices with their start and end apart: 4 -> 5, of which waited for: 3 -> 4; matrix products, arithmetic and copies ran while one was open for 0% -> 0% of each run, Pallas kernels for 3% -> 4%
where the time goes in v3:
time: 159 us
  blocking collectives  99.5 us (63%)
  starting transfers between devices  24.7 us (16%)
  Pallas kernels  23 us (14%)
  waiting for transfers between devices  10.8 us (7%)
    all_to_all x5, blocking collectives, exchange(): return lax.all_to_all(value, axis, 0, 0, axis_index_groups=groups)  99.5 us
    pallas_call x9, Pallas kernels, call(): pl.pallas_call(kernel, out_shape=[jax.ShapeDtypeStruct(*o) for o in out],...  23 us
    all_to_all x1, starting transfers between devices, exchange(): return lax.all_to_all(value, axis, 0, 0, axis_index_groups=groups)  16.7 us
    ppermute x4, starting transfers between devices, swap(): return lax.ppermute(value, 'col', [(q, q ^ 1) for q in range(COLS)])  7.98 us
    all_to_all x1, waiting for transfers between devices, exchange(): return lax.all_to_all(value, axis, 0, 0, axis_index_groups=groups)  7.51 us
    ppermute x4, waiting for transfers between devices, swap(): return lax.ppermute(value, 'col', [(q, q ^ 1) for q in range(COLS)])  3.31 us
  transfers between devices with their start and end apart: 5, of which 4 were waited for; matrix products, arithmetic and copies ran while one was open for 0% of the time, Pallas kernels for 4%

profile of v3, /device:TPU:8, one launch (start us, length us, event | category | flops | bytes accessed | tf_op | source)
XLA Modules:
  0.0 158.9 jit_solution(10616319357876436628)
XLA Ops:
  0.6 2.1 %collective-permute-start.1 = (bf16[1536,256]{1,0:T(8,128)(2,1)}, bf16[1536,256]{1,0:T(8,128)(2,1)S(1)}, u32[]{:S(2)}, u32[]{:S(2)}) collective-permute-start(bf16[1536,256]{1,0:T(8,128)(2,1)} %probes.1), channel_id=1, source_target_pairs={{0,1},{1,0},{2,3},{3,2},{4,5},{5,4},{6,7},{7,6},{8,9},{9,8},{10,11... | collective-permute-start | bytes 2359304 | tf_op jit(solution)/shard_map/ppermute | solution.py:320
  2.7 0.1 pad_add_fusion.place
  2.8 3.1 %shard_map.60 = bf16[640,128]{1,0:T(8,128)(2,1)} custom-call(s32[2]{0:T(128)S(1)} %pad_add_fusion.place, bf16[3,24,4096]{2,1,0:T(8,128)(2,1)} %bitcast.20), custom_call_target="tpu_custom_call" | custom-call | tf_op jit(solution)/shard_map/pallas_call | solution.py:297
  5.9 16.7 %all-to-all-start = ((bf16[64,5,2,128]{3,2,1,0:T(2,128)(2,1)}), bf16[64,5,2,128]{3,2,1,0:T(2,128)(2,1)S(1)}, u32[]{:S(2)}, u32[]{:S(2)}) async-start(bf16[64,5,2,128]{3,2,1,0:T(2,128)(2,1)} %bitcast.4), calls=%async_computation | async-start | bytes 327680 | tf_op jit(solution)/shard_map/all_to_all | solution.py:312
  22.6 1.9 %collective-permute-start = (bf16[3,64,512]{2,1,0:T(8,128)(2,1)S(1)}, bf16[3,64,512]{2,1,0:T(8,128)(2,1)S(1)}, u32[]{:S(2)}, u32[]{:S(2)}) collective-permute-start(bf16[3,64,512]{2,1,0:T(8,128)(2,1)S(1)} %bitcast.14), channel_id=1, source_target_pairs={{0,1},{1,0},{2,3},{3,2},{4,5},{5,4},{6,7},{7,6},{8,9},{9,8},{10,11... | collective-permute-start | bytes 589832 | tf_op jit(solution)/shard_map/ppermute | solution.py:320
  24.6 1.4 collective-permute-done.right_other
  26.0 2.3 %shard_map.59 = bf16[4,192,384]{2,1,0:T(8,128)(2,1)S(1)} custom-call(s32[2]{0:T(128)S(1)} %pad_add_fusion.place, f32[9,9]{1,0:T(8,128)S(1)} %copy-done.2, bf16[3,64,512]{2,1,0:T(8,128)(2,1)S(1)} %bitcast.15, bf16[1536,256]{1,0:T(8,128)(2,1)S(1)} %copy-done.1, bf16[3,64,512]{2,1,0:T(8,128)(2,1)S(1)} %collective-permute-done.right_other, ...), custom_call_target="tpu_custom_call" | custom-call | tf_op jit(solution)/shard_map/pallas_call | solution.py:297
  28.3 7.5 %all-to-all-done = bf16[64,5,2,128]{3,2,1,0:T(2,128)(2,1)S(1)} async-done(((bf16[64,5,2,128]{3,2,1,0:T(2,128)(2,1)}), bf16[64,5,2,128]{3,2,1,0:T(2,128)(2,1)S(1)}, u32[]{:S(2)}, u32[]{:S(2)}) %all-to-all-start) | async-done | bytes 163872 | tf_op jit(solution)/shard_map/all_to_all | solution.py:312
  35.8 13.3 %all_to_all.30.weight = bf16[4,192,384]{2,1,0:T(8,128)(2,1)S(1)} all-to-all(bf16[4,192,384]{2,1,0:T(8,128)(2,1)S(1)} %shard_map.59), channel_id=1, replica_groups={{0,2,4,6},{1,3,5,7},{8,10,12,14},{9,11,13,15},{16,18,20,22},{17,19,21,2..., dimensions={0} | all-to-all | bytes 1179648 | tf_op jit(solution)/shard_map/all_to_all | solution.py:312
  49.1 0.9 shard_map.61
  50.0 20.4 %all_to_all.31 = bf16[64,9,2,128]{3,2,1,0:T(2,128)(2,1)S(1)} all-to-all(bf16[64,9,2,128]{3,2,1,0:T(2,128)(2,1)S(1)} %bitcast.18), channel_id=1, replica_groups=mesh['row'=64,'col'=8] {'row'}, dimensions={0} | all-to-all | bytes 589824 | tf_op jit(solution)/shard_map/all_to_all | solution.py:312
  70.4 0.1 shard_map.62
  70.4 19.2 %all_to_all.32 = bf16[64,9,2,128]{3,2,1,0:T(2,128)(2,1)S(1)} all-to-all(bf16[64,9,2,128]{3,2,1,0:T(2,128)(2,1)S(1)} %bitcast.19), channel_id=1, replica_groups=mesh['row'=64,'col'=8] {'row'}, dimensions={0} | all-to-all | bytes 589824 | tf_op jit(solution)/shard_map/all_to_all | solution.py:312
  89.6 1.9 %collective-permute-start.2 = (bf16[1152,128]{1,0:T(8,128)(2,1)S(1)}, bf16[1152,128]{1,0:T(8,128)(2,1)S(1)}, u32[]{:S(2)}, u32[]{:S(2)}) collective-permute-start(bf16[1152,128]{1,0:T(8,128)(2,1)S(1)} %bitcast.10), channel_id=1, source_target_pairs={{0,1},{1,0},{2,3},{3,2},{4,5},{5,4},{6,7},{7,6},{8,9},{9,8},{10,11... | collective-permute-start | bytes 884744 | tf_op jit(solution)/shard_map/ppermute | solution.py:320
  91.5 1.2 shard_map.63.value
  92.7 0.4 collective-permute-done.2.other_in
  93.1 1.0 shard_map.64
  94.1 17.7 %all_to_all.33.pieces = bf16[4,984,128]{2,1,0:T(8,128)(2,1)S(1)} all-to-all(bf16[4,984,128]{2,1,0:T(8,128)(2,1)S(1)} %shard_map.64), channel_id=1, replica_groups={{0,2,4,6},{1,3,5,7},{8,10,12,14},{9,11,13,15},{16,18,20,22},{17,19,21,2..., dimensions={0} | all-to-all | bytes 2015232 | tf_op jit(solution)/shard_map/all_to_all | solution.py:312
  111.7 0.2 shard_map.65.mine
  111.9 2.1 %collective-permute-start.3 = (bf16[1632,128]{1,0:T(8,128)(2,1)S(1)}, bf16[1632,128]{1,0:T(8,128)(2,1)S(1)}, u32[]{:S(2)}, u32[]{:S(2)}) collective-permute-start(bf16[1632,128]{1,0:T(8,128)(2,1)S(1)} %shard_map.65.mine), channel_id=1, source_target_pairs={{0,1},{1,0},{2,3},{3,2},{4,5},{5,4},{6,7},{7,6},{8,9},{9,8},{10,11... | collective-permute-start | bytes 1253384 | tf_op jit(solution)/shard_map/ppermute | solution.py:320
  114.0 1.5 collective-permute-done.3.other
  115.5 13.0 %shard_map.66 = (f32[72,256]{1,0:T(8,128)}, bf16[64,8,768]{2,1,0:T(8,128)(2,1)S(1)}) custom-call(s32[2]{0:T(128)S(1)} %pad_add_fusion.place, bf16[1632,128]{1,0:T(8,128)(2,1)S(1)} %shard_map.65.mine, bf16[1632,128]{1,0:T(8,128)(2,1)S(1)} %collective-permute-done.3.other, bf16[3,64,512]{2,1,0:T(8,128)(2,1)S(1)} %bitcast.16), custom_call_target="tpu_custom_call" | custom-call | tf_op jit(solution)/shard_map/pallas_call | solution.py:297
  128.5 29.0 %all_to_all.34.pieces = bf16[64,8,768]{2,1,0:T(8,128)(2,1)S(1)} all-to-all(bf16[64,8,768]{2,1,0:T(8,128)(2,1)S(1)} %get-tuple-element.17), channel_id=1, replica_groups=mesh['row'=64,'col'=8] {'row'}, dimensions={0} | all-to-all | bytes 1572864 | tf_op jit(solution)/shard_map/all_to_all | solution.py:312
  157.5 1.4 shard_map.67
  (7 shorter events, 0.0 us)
Async XLA Ops:
  0.6 25.3 %copy-start.1 = (bf16[1536,256]{1,0:T(8,128)(2,1)S(1)}, bf16[1536,256]{1,0:T(8,128)(2,1)}, u32[]{:S(2)}) copy-start(bf16[1536,256]{1,0:T(8,128)(2,1)} %probes.1) | copy-start | bytes 2359300
  0.6 25.3 %collective-permute-start.1 = (bf16[1536,256]{1,0:T(8,128)(2,1)}, bf16[1536,256]{1,0:T(8,128)(2,1)S(1)}, u32[]{:S(2)}, u32[]{:S(2)}) collective-permute-start(bf16[1536,256]{1,0:T(8,128)(2,1)} %probes.1), channel_id=1, source_target_pairs={{0,1},{1,0},{2,3},{3,2},{4,5},{5,4},{6,7},{7,6},{8,9},{9,8},{10,11... | collective-permute-start | bytes 2359304 | tf_op jit(solution)/shard_map/ppermute | solution.py:320
  5.9 16.8 %copy-start = (bf16[64,3,512]{2,0,1:T(8,128)(2,1)S(1)}, bf16[64,3,512]{2,0,1:T(8,128)(2,1)}, u32[]{:S(2)}) copy-start(bf16[64,3,512]{2,0,1:T(8,128)(2,1)} %param.5) | copy-start | bytes 589828
  5.9 20.1 %copy-start.2 = (f32[9,9]{1,0:T(8,128)S(1)}, f32[9,9]{1,0:T(8,128)}, u32[]{:S(2)}) copy-start(f32[9,9]{1,0:T(8,128)} %gate.3) | copy-start | bytes 976
  5.9 29.9 %all-to-all-start = ((bf16[64,5,2,128]{3,2,1,0:T(2,128)(2,1)}), bf16[64,5,2,128]{3,2,1,0:T(2,128)(2,1)S(1)}, u32[]{:S(2)}, u32[]{:S(2)}) async-start(bf16[64,5,2,128]{3,2,1,0:T(2,128)(2,1)} %bitcast.4), calls=%async_computation | async-start | bytes 327680 | tf_op jit(solution)/shard_map/all_to_all | solution.py:312
  22.6 3.3 %collective-permute-start = (bf16[3,64,512]{2,1,0:T(8,128)(2,1)S(1)}, bf16[3,64,512]{2,1,0:T(8,128)(2,1)S(1)}, u32[]{:S(2)}, u32[]{:S(2)}) collective-permute-start(bf16[3,64,512]{2,1,0:T(8,128)(2,1)S(1)} %bitcast.14), channel_id=1, source_target_pairs={{0,1},{1,0},{2,3},{3,2},{4,5},{5,4},{6,7},{7,6},{8,9},{9,8},{10,11... | collective-permute-start | bytes 589832 | tf_op jit(solution)/shard_map/ppermute | solution.py:320
  89.6 3.5 %collective-permute-start.2 = (bf16[1152,128]{1,0:T(8,128)(2,1)S(1)}, bf16[1152,128]{1,0:T(8,128)(2,1)S(1)}, u32[]{:S(2)}, u32[]{:S(2)}) collective-permute-start(bf16[1152,128]{1,0:T(8,128)(2,1)S(1)} %bitcast.10), channel_id=1, source_target_pairs={{0,1},{1,0},{2,3},{3,2},{4,5},{5,4},{6,7},{7,6},{8,9},{9,8},{10,11... | collective-permute-start | bytes 884744 | tf_op jit(solution)/shard_map/ppermute | solution.py:320
  111.9 3.7 %collective-permute-start.3 = (bf16[1632,128]{1,0:T(8,128)(2,1)S(1)}, bf16[1632,128]{1,0:T(8,128)(2,1)S(1)}, u32[]{:S(2)}, u32[]{:S(2)}) collective-permute-start(bf16[1632,128]{1,0:T(8,128)(2,1)S(1)} %shard_map.65.mine), channel_id=1, source_target_pairs={{0,1},{1,0},{2,3},{3,2},{4,5},{5,4},{6,7},{7,6},{8,9},{9,8},{10,11... | collective-permute-start | bytes 1253384 | tf_op jit(solution)/shard_map/ppermute | solution.py:320

commit v4 on v3

--- a/solution.py
+++ b/solution.py
@@ -27,57 +27,45 @@
     return jnp.where(column == 3 * b + t, 1.0, 0.0).astype(BF16)
 
 
-def left_kernel(place, left, left_out, rows, lines, arrived):
-    x = place[1] // 2
-    start = pl.multiple_of(8 * (x // 2), 8)
-    copies = [
-        pltpu.make_async_copy(
-            left.at[:, pl.ds(start, 16), 1024 * part : 1024 * part + 1024],
-            rows.at[part],
-            arrived.at[part],
-        )
-        for part in range(4)
-    ]
-    for copy in copies:
-        copy.start()
-    row, column, lane = iota((16, 48), 0), iota((16, 48), 1), iota((16, 128), 1)
-    picks = []
+def left_kernel(place, left, left_out, lines):
+    row, column, lane = iota((16, 72), 0), iota((16, 72), 1), iota((16, 128), 1)
+    sides = []
     for h in range(2):
         line = 2 * row + h
         photon = jnp.where(line < 6, 0, jnp.where(line < 12, 1, 2))
-        chosen = (column == photon * 16 + 6 * x - start + line - 6 * photon) & (line < 18)
-        picks.append(jnp.where(chosen, 1.0, 0.0).astype(BF16))
-    for part in range(4):
-        copies[part].wait()
-        sides = [dot(pick, rows[part].reshape(48, 1024)) for pick in picks]
-        for pair in range(8):
-            even, odd = (side[:, 128 * pair : 128 * pair + 128] for side in sides)
-            first = jnp.where(lane < 64, even, pltpu.roll(odd, 64, 1))
-            second = jnp.where(lane < 64, pltpu.roll(even, 64, 1), odd)
-            at = 160 * part + 20 * pair
-            lines[at : at + 10, :] = first[:10]
-            lines[at + 10 : at + 20, :] = second[:10]
+        chosen = (column == photon * 24 + 6 * (place[1] // 2) + line - 6 * photon) & (line < 18)
+        sides.append(dot(jnp.where(chosen, 1.0, 0.0).astype(BF16), left[...].reshape(72, 4096)))
+    for pair in range(ROWS // 2):
+        even, odd = (side[:, 128 * pair : 128 * pair + 128] for side in sides)
+        first = jnp.where(lane < 64, even, pltpu.roll(odd, 64, 1))
+        second = jnp.where(lane < 64, pltpu.roll(even, 64, 1), odd)
+        lines[20 * pair : 20 * pair + 10, :] = first[:10]
+        lines[20 * pair + 10 : 20 * pair + 20, :] = second[:10]
     left_out[...] = lines[...].astype(BF16)
 
 
-def first_kernel(place, gate, right, probes, right_other, probes_other, weight_out, product):
-    half = pl.ds(pl.multiple_of(128 * (place[1] % 2), 128), 128)
+def first_kernel(place, gate, right, probes, kept, sent, product):
+    core = place[1] % 2
+    wide = right[...].reshape(192, 512)
     for t in range(3):
         pick = stride_three(t, False)
-        total = jnp.zeros((192, 128), F32)
-        for side, probe in ((right, probes), (right_other, probes_other)):
-            own = [dot(pick, probe[384 * j : 384 * j + 384, half]).astype(BF16) for j in range(4)]
-            total = total + dot(side[...].reshape(192, 512), jnp.concatenate(own, axis=0))
-        product[t] = total
-    for up in range(3):
-        for s in range(3):
-            total = jnp.zeros((64, 128), F32)
-            for tp in range(3):
-                for t in range(3):
-                    total = total + gate[3 * s + t, 3 * up + tp] * product[t, 64 * tp : 64 * tp + 64, :]
-            total = total.astype(BF16)
-            for x in range(4):
-                weight_out[x, 64 * up : 64 * up + 64, 128 * s : 128 * s + 128] = total
+        own = [dot(pick, probes[384 * j : 384 * j + 384, :]).astype(BF16) for j in range(4)]
+        product[t] = dot(wide, jnp.concatenate(own, axis=0))
+    for out, k in ((sent, 1 - core), (kept, core)):
+        half = pl.ds(pl.multiple_of(128 * k, 128), 128)
+        for up in range(3):
+            for s in range(3):
+                total = jnp.zeros((64, 128), F32)
+                for tp in range(3):
+                    for t in range(3):
+                        total = total + gate[3 * s + t, 3 * up + tp] * product[t, 64 * tp : 64 * tp + 64, half]
+                out[64 * up : 64 * up + 64, 128 * s : 128 * s + 128] = total
+
+
+def weight_kernel(kept, received, out):
+    total = (kept[...] + received[...]).astype(BF16)
+    for x in range(4):
+        out[x] = total
 
 
 def sketch_kernel(left_in, weight, sketch_out, left_rows, wide_left, high, low, wide_sketch):
@@ -291,15 +279,13 @@
 INTERPRET = False
 
 
-def call(kernel, out, *args, smem=0, far=0, scratch=(), copies=0):
-    near = len(args) - smem - far
-    shapes = [pltpu.VMEM(*s) for s in scratch]
+def call(kernel, out, *args, smem=0, scratch=()):
     return pl.pallas_call(
         kernel,
         out_shape=[jax.ShapeDtypeStruct(*o) for o in out],
-        in_specs=[SMEM] * smem + [VMEM] * near + [pl.BlockSpec(memory_space=pltpu.HBM)] * far,
+        in_specs=[SMEM] * smem + [VMEM] * (len(args) - smem),
         out_specs=[VMEM] * len(out),
-        scratch_shapes=shapes + ([pltpu.SemaphoreType.DMA((copies,))] if copies else []),
+        scratch_shapes=[pltpu.VMEM(*s) for s in scratch],
         compiler_params=pltpu.CompilerParams(vmem_limit_bytes=48 * 1024 * 1024),
         interpret=INTERPRET,
     )(*args)
@@ -324,25 +310,17 @@
     place = jnp.stack([lax.axis_index("row"), lax.axis_index("col")]).astype(jnp.int32)
     left = left_site.transpose(1, 0, 2)
     right = right_site.transpose(1, 0, 2)
-    (left_out,) = call(
-        left_kernel,
-        [((ROWS * 10, 128), BF16)],
-        place, pltpu.with_memory_space_constraint(left, pltpu.HBM),
-        smem=1,
-        far=1,
-        scratch=[((4, 3, 16, 1024), BF16), ((ROWS * 10, 128), F32)],
-        copies=4,
-    )
+    (left_out,) = call(left_kernel, [((ROWS * 10, 128), BF16)], place, left, smem=1, scratch=[((ROWS * 10, 128), F32)])
     left_in = exchange_lines(left_out, 10)
-    right_other = swap(right)
-    probes_other = swap(probes_matrix)
-    (weight,) = call(
+    kept, sent = call(
         first_kernel,
-        [((4, 192, 384), BF16)],
-        place, gate, right, probes_matrix, right_other, probes_other,
+        [((192, 384), F32), ((192, 384), F32)],
+        place, gate, right, probes_matrix,
         smem=2,
-        scratch=[((3, 192, 128), F32)],
-    )
+        scratch=[((3, 192, 256), F32)],
+    )
+    received = swap(sent)
+    (weight,) = call(weight_kernel, [((4, 192, 384), BF16)], kept, received)
     weight, left_in = lax.optimization_barrier((weight, left_in))
     weight = exchange(weight, "col", LINES_OF_X)
     sketch, left_rows = call(

time: 159 us -> 157 us (0.987)
  starting transfers between devices: 24.7 us -> 22.6 us
  Pallas kernels: 23 us -> 21.3 us
    ppermute x4 -> x3, starting transfers between devices: 7.98 us -> 5.93 us  [swap(): return lax.ppermute(value, 'col', [(q, q ^ 1) for q in range(COLS)])]
    pallas_call x9 -> x10, Pallas kernels: 23 us -> 21.3 us  [call(): pl.pallas_call(kernel, out_shape=[jax.ShapeDtypeStruct(*o) for o in out],...]
    ppermute x4 -> x3, waiting for transfers between devices: 3.31 us -> 3.45 us  [swap(): return lax.ppermute(value, 'col', [(q, q ^ 1) for q in range(COLS)])]
  transfers between devices with their start and end apart: 5 -> 4, of which waited for: 4 -> 4; matrix products, arithmetic and copies ran while one was open for 0% -> 0% of each run, Pallas kernels for 4% -> 2%
where the time goes in v4:
time: 157 us; the launch traced here: 156 us
  blocking collectives  100 us (64%)
  starting transfers between devices  22.6 us (14%)
  Pallas kernels  21.3 us (14%)
  waiting for transfers between devices  10.4 us (7%)
    all_to_all x5, blocking collectives, exchange(): return lax.all_to_all(value, axis, 0, 0, axis_index_groups=groups)  100 us
    pallas_call x10, Pallas kernels, call(): pl.pallas_call(kernel, out_shape=[jax.ShapeDtypeStruct(*o) for o in out],...  21.3 us
    all_to_all x1, starting transfers between devices, exchange(): return lax.all_to_all(value, axis, 0, 0, axis_index_groups=groups)  16.7 us
    all_to_all x1, waiting for transfers between devices, exchange(): return lax.all_to_all(value, axis, 0, 0, axis_index_groups=groups)  6.91 us
    ppermute x3, starting transfers between devices, swap(): return lax.ppermute(value, 'col', [(q, q ^ 1) for q in range(COLS)])  5.93 us
    ppermute x3, waiting for transfers between devices, swap(): return lax.ppermute(value, 'col', [(q, q ^ 1) for q in range(COLS)])  3.45 us
  transfers between devices with their start and end apart: 4, of which 4 were waited for; matrix products, arithmetic and copies ran while one was open for 0% of the time, Pallas kernels for 2%

profile of v4, /device:TPU:8, one launch (start us, length us, event | category | flops | bytes accessed | tf_op | source)
XLA Modules:
  0.0 156.4 jit_solution(2010439107079949174)
XLA Ops:
  0.6 0.1 pad_add_fusion.place
  0.7 1.1 copy-done.2
  1.8 1.6 %shard_map.61 = bf16[640,128]{1,0:T(8,128)(2,1)} custom-call(s32[2]{0:T(128)S(1)} %pad_add_fusion.place, bf16[3,24,4096]{2,1,0:T(8,128)(2,1)S(1)} %bitcast.17), custom_call_target="tpu_custom_call" | custom-call | tf_op jit(solution)/shard_map/pallas_call | solution.py:283
  3.5 16.7 %all-to-all-start = ((bf16[64,5,2,128]{3,2,1,0:T(2,128)(2,1)}), bf16[64,5,2,128]{3,2,1,0:T(2,128)(2,1)S(1)}, u32[]{:S(2)}, u32[]{:S(2)}) async-start(bf16[64,5,2,128]{3,2,1,0:T(2,128)(2,1)} %bitcast.4), calls=%async_computation | async-start | bytes 327680 | tf_op jit(solution)/shard_map/all_to_all | solution.py:298
  20.2 2.0 %shard_map.59 = (f32[192,384]{1,0:T(8,128)S(1)}, f32[192,384]{1,0:T(8,128)S(1)}) custom-call(s32[2]{0:T(128)S(1)} %pad_add_fusion.place, f32[9,9]{1,0:T(8,128)S(1)} %copy-done.3, bf16[3,64,512]{2,1,0:T(8,128)(2,1)S(1)} %bitcast.14, bf16[1536,256]{1,0:T(8,128)(2,1)S(1)} %copy-done.1), custom_call_target="tpu_custom_call" | custom-call | tf_op jit(solution)/shard_map/pallas_call | solution.py:283
  22.2 1.9 %collective-permute-start = (f32[192,384]{1,0:T(8,128)S(1)}, f32[192,384]{1,0:T(8,128)S(1)}, u32[]{:S(2)}, u32[]{:S(2)}) collective-permute-start(f32[192,384]{1,0:T(8,128)S(1)} %get-tuple-element.13), channel_id=1, source_target_pairs={{0,1},{1,0},{2,3},{3,2},{4,5},{5,4},{6,7},{7,6},{8,9},{9,8},{10,11... | collective-permute-start | bytes 884744 | tf_op jit(solution)/shard_map/ppermute | solution.py:306
  24.2 1.5 collective-permute-done.received
  25.8 6.9 %all-to-all-done = bf16[64,5,2,128]{3,2,1,0:T(2,128)(2,1)S(1)} async-done(((bf16[64,5,2,128]{3,2,1,0:T(2,128)(2,1)}), bf16[64,5,2,128]{3,2,1,0:T(2,128)(2,1)S(1)}, u32[]{:S(2)}, u32[]{:S(2)}) %all-to-all-start) | async-done | bytes 163872 | tf_op jit(solution)/shard_map/all_to_all | solution.py:298
  32.7 12.7 %all_to_all.30.weight = bf16[4,192,384]{2,1,0:T(8,128)(2,1)S(1)} all-to-all(bf16[4,192,384]{2,1,0:T(8,128)(2,1)S(1)} %shard_map.60), channel_id=1, replica_groups={{0,2,4,6},{1,3,5,7},{8,10,12,14},{9,11,13,15},{16,18,20,22},{17,19,21,2..., dimensions={0} | all-to-all | bytes 1179648 | tf_op jit(solution)/shard_map/all_to_all | solution.py:298
  45.4 0.9 shard_map.62
  46.2 21.6 %all_to_all.31 = bf16[64,9,2,128]{3,2,1,0:T(2,128)(2,1)S(1)} all-to-all(bf16[64,9,2,128]{3,2,1,0:T(2,128)(2,1)S(1)} %bitcast.18), channel_id=1, replica_groups=mesh['row'=64,'col'=8] {'row'}, dimensions={0} | all-to-all | bytes 589824 | tf_op jit(solution)/shard_map/all_to_all | solution.py:298
  67.8 0.1 shard_map.63
  67.9 19.2 %all_to_all.32 = bf16[64,9,2,128]{3,2,1,0:T(2,128)(2,1)S(1)} all-to-all(bf16[64,9,2,128]{3,2,1,0:T(2,128)(2,1)S(1)} %bitcast.19), channel_id=1, replica_groups=mesh['row'=64,'col'=8] {'row'}, dimensions={0} | all-to-all | bytes 589824 | tf_op jit(solution)/shard_map/all_to_all | solution.py:298
  87.1 1.9 %collective-permute-start.1 = (bf16[1152,128]{1,0:T(8,128)(2,1)S(1)}, bf16[1152,128]{1,0:T(8,128)(2,1)S(1)}, u32[]{:S(2)}, u32[]{:S(2)}) collective-permute-start(bf16[1152,128]{1,0:T(8,128)(2,1)S(1)} %bitcast.10), channel_id=1, source_target_pairs={{0,1},{1,0},{2,3},{3,2},{4,5},{5,4},{6,7},{7,6},{8,9},{9,8},{10,11... | collective-permute-start | bytes 884744 | tf_op jit(solution)/shard_map/ppermute | solution.py:306
  89.0 1.2 shard_map.64.value
  90.2 0.4 collective-permute-done.1.other_in
  90.5 1.0 shard_map.65
  91.6 17.6 %all_to_all.33.pieces = bf16[4,984,128]{2,1,0:T(8,128)(2,1)S(1)} all-to-all(bf16[4,984,128]{2,1,0:T(8,128)(2,1)S(1)} %shard_map.65), channel_id=1, replica_groups={{0,2,4,6},{1,3,5,7},{8,10,12,14},{9,11,13,15},{16,18,20,22},{17,19,21,2..., dimensions={0} | all-to-all | bytes 2015232 | tf_op jit(solution)/shard_map/all_to_all | solution.py:298
  109.2 0.2 shard_map.66.mine
  109.4 2.1 %collective-permute-start.2 = (bf16[1632,128]{1,0:T(8,128)(2,1)S(1)}, bf16[1632,128]{1,0:T(8,128)(2,1)S(1)}, u32[]{:S(2)}, u32[]{:S(2)}) collective-permute-start(bf16[1632,128]{1,0:T(8,128)(2,1)S(1)} %shard_map.66.mine), channel_id=1, source_target_pairs={{0,1},{1,0},{2,3},{3,2},{4,5},{5,4},{6,7},{7,6},{8,9},{9,8},{10,11... | collective-permute-start | bytes 1253384 | tf_op jit(solution)/shard_map/ppermute | solution.py:306
  111.5 1.5 collective-permute-done.2.other
  113.0 13.0 %shard_map.67 = (f32[72,256]{1,0:T(8,128)}, bf16[64,8,768]{2,1,0:T(8,128)(2,1)S(1)}) custom-call(s32[2]{0:T(128)S(1)} %pad_add_fusion.place, bf16[1632,128]{1,0:T(8,128)(2,1)S(1)} %shard_map.66.mine, bf16[1632,128]{1,0:T(8,128)(2,1)S(1)} %collective-permute-done.2.other, bf16[3,64,512]{2,1,0:T(8,128)(2,1)S(1)} %bitcast.15), custom_call_target="tpu_custom_call" | custom-call | tf_op jit(solution)/shard_map/pallas_call | solution.py:283
  126.0 29.0 %all_to_all.34.pieces = bf16[64,8,768]{2,1,0:T(8,128)(2,1)S(1)} all-to-all(bf16[64,8,768]{2,1,0:T(8,128)(2,1)S(1)} %get-tuple-element.21), channel_id=1, replica_groups=mesh['row'=64,'col'=8] {'row'}, dimensions={0} | all-to-all | bytes 1572864 | tf_op jit(solution)/shard_map/all_to_all | solution.py:298
  155.0 1.4 shard_map.68
  (8 shorter events, 0.1 us)
Async XLA Ops:
  0.6 19.6 %copy-start.1 = (bf16[1536,256]{1,0:T(8,128)(2,1)S(1)}, bf16[1536,256]{1,0:T(8,128)(2,1)}, u32[]{:S(2)}) copy-start(bf16[1536,256]{1,0:T(8,128)(2,1)} %probes.1) | copy-start | bytes 2359300
  0.7 1.1 copy-start.2
  3.5 16.7 %copy-start = (bf16[64,3,512]{2,0,1:T(8,128)(2,1)S(1)}, bf16[64,3,512]{2,0,1:T(8,128)(2,1)}, u32[]{:S(2)}) copy-start(bf16[64,3,512]{2,0,1:T(8,128)(2,1)} %param.5) | copy-start | bytes 589828
  3.5 16.7 %copy-start.3 = (f32[9,9]{1,0:T(8,128)S(1)}, f32[9,9]{1,0:T(8,128)}, u32[]{:S(2)}) copy-start(f32[9,9]{1,0:T(8,128)} %gate.3) | copy-start | bytes 976
  3.5 29.2 %all-to-all-start = ((bf16[64,5,2,128]{3,2,1,0:T(2,128)(2,1)}), bf16[64,5,2,128]{3,2,1,0:T(2,128)(2,1)S(1)}, u32[]{:S(2)}, u32[]{:S(2)}) async-start(bf16[64,5,2,128]{3,2,1,0:T(2,128)(2,1)} %bitcast.4), calls=%async_computation | async-start | bytes 327680 | tf_op jit(solution)/shard_map/all_to_all | solution.py:298
  22.2 3.5 %collective-permute-start = (f32[192,384]{1,0:T(8,128)S(1)}, f32[192,384]{1,0:T(8,128)S(1)}, u32[]{:S(2)}, u32[]{:S(2)}) collective-permute-start(f32[192,384]{1,0:T(8,128)S(1)} %get-tuple-element.13), channel_id=1, source_target_pairs={{0,1},{1,0},{2,3},{3,2},{4,5},{5,4},{6,7},{7,6},{8,9},{9,8},{10,11... | collective-permute-start | bytes 884744 | tf_op jit(solution)/shard_map/ppermute | solution.py:306
  87.1 3.5 %collective-permute-start.1 = (bf16[1152,128]{1,0:T(8,128)(2,1)S(1)}, bf16[1152,128]{1,0:T(8,128)(2,1)S(1)}, u32[]{:S(2)}, u32[]{:S(2)}) collective-permute-start(bf16[1152,128]{1,0:T(8,128)(2,1)S(1)} %bitcast.10), channel_id=1, source_target_pairs={{0,1},{1,0},{2,3},{3,2},{4,5},{5,4},{6,7},{7,6},{8,9},{9,8},{10,11... | collective-permute-start | bytes 884744 | tf_op jit(solution)/shard_map/ppermute | solution.py:306
  109.4 3.7 %collective-permute-start.2 = (bf16[1632,128]{1,0:T(8,128)(2,1)S(1)}, bf16[1632,128]{1,0:T(8,128)(2,1)S(1)}, u32[]{:S(2)}, u32[]{:S(2)}) collective-permute-start(bf16[1632,128]{1,0:T(8,128)(2,1)S(1)} %shard_map.66.mine), channel_id=1, source_target_pairs={{0,1},{1,0},{2,3},{3,2},{4,5},{5,4},{6,7},{7,6},{8,9},{9,8},{10,11... | collective-permute-start | bytes 1253384 | tf_op jit(solution)/shard_map/ppermute | solution.py:306

commit v5 on v4

--- a/solution.py
+++ b/solution.py
@@ -41,7 +41,7 @@
         second = jnp.where(lane < 64, pltpu.roll(even, 64, 1), odd)
         lines[20 * pair : 20 * pair + 10, :] = first[:10]
         lines[20 * pair + 10 : 20 * pair + 20, :] = second[:10]
-    left_out[...] = lines[...].astype(BF16)
+    left_out[...] = lines[: ROWS * 10, :].astype(BF16)
 
 
 def first_kernel(place, gate, right, probes, kept, sent, product):
@@ -94,13 +94,13 @@
     total = pieces[:144, :].astype(F32)
     for k in range(1, 8):
         total = total + pieces[144 * k : 144 * k + 144, :].astype(F32)
-    four[...] = total[:72] + total[72:]
+    four[:72, :] = total[:72] + total[72:]
     total = four[0:18, :] + four[18:36, :] + four[36:54, :] + four[54:72, :]
     own[:18, :] = total.astype(BF16)
     own[18:, :] = jnp.zeros((6, 128), BF16)
     for k in range(8):
         many[18 * k : 18 * k + 18, :] = total
-    total = many[...].astype(BF16)
+    total = many[:144, :].astype(BF16)
     for k in range(8):
         out[144 * k : 144 * k + 144, :] = total
 
@@ -234,7 +234,7 @@
             rows = pieces[1536 + 24 * x : 1560 + 24 * x, :].astype(F32)
             sketch[18 * x : 18 * x + 18, half] = rows[:18]
     high, low = split(inverse[...])
-    own = sketch[...].astype(BF16)
+    own = sketch[:72, :].astype(BF16)
     basis_out[...] = dot(own, high, ((1,), (1,))) + dot(own, low, ((1,), (1,)))
     for part in range(2):
         for pieces, half, _ in halves:
@@ -310,7 +310,9 @@
     place = jnp.stack([lax.axis_index("row"), lax.axis_index("col")]).astype(jnp.int32)
     left = left_site.transpose(1, 0, 2)
     right = right_site.transpose(1, 0, 2)
-    (left_out,) = call(left_kernel, [((ROWS * 10, 128), BF16)], place, left, smem=1, scratch=[((ROWS * 10, 128), F32)])
+    (left_out,) = call(
+        left_kernel, [((ROWS * 10, 128), BF16)], place, left, smem=1, scratch=[((ROWS * 10 + 8, 128), F32)]
+    )
     left_in = exchange_lines(left_out, 10)
     kept, sent = call(
         first_kernel,
@@ -334,7 +336,7 @@
         total_kernel,
         [((24, 128), BF16), ((ROWS * 18, 128), BF16)],
         sketch,
-        scratch=[((72, 128), F32), ((144, 128), F32)],
+        scratch=[((80, 128), F32), ((152, 128), F32)],
     )
     sketch = exchange_lines(sketch, 18)
     other = swap(sketch)
@@ -360,7 +362,7 @@
         place, value, swap(value), right,
         smem=1,
         scratch=[
-            ((256, 256), F32), ((256, 256), F32), ((256, 256), F32), ((72, 256), F32),
+            ((256, 256), F32), ((256, 256), F32), ((256, 256), F32), ((80, 256), F32),
             ((2, 3, 192, 256), BF16), ((256, 1536), F32),
         ],
     )

time: 157 us -> 157 us (level)
  no operation moved by 1% of the time
where the time goes in v5:
time: 157 us; the launch traced here: 156 us
  blocking collectives  100 us (64%)
  starting transfers between devices  22.6 us (14%)
  Pallas kernels  21.3 us (14%)
  waiting for transfers between devices  10.4 us (7%)
    all_to_all x5, blocking collectives, exchange(): return lax.all_to_all(value, axis, 0, 0, axis_index_groups=groups)  100 us
    pallas_call x10, Pallas kernels, call(): pl.pallas_call(kernel, out_shape=[jax.ShapeDtypeStruct(*o) for o in out],...  21.3 us
    all_to_all x1, starting transfers between devices, exchange(): return lax.all_to_all(value, axis, 0, 0, axis_index_groups=groups)  16.7 us
    all_to_all x1, waiting for transfers between devices, exchange(): return lax.all_to_all(value, axis, 0, 0, axis_index_groups=groups)  6.91 us
    ppermute x3, starting transfers between devices, swap(): return lax.ppermute(value, 'col', [(q, q ^ 1) for q in range(COLS)])  5.93 us
    ppermute x3, waiting for transfers between devices, swap(): return lax.ppermute(value, 'col', [(q, q ^ 1) for q in range(COLS)])  3.45 us
  transfers between devices with their start and end apart: 4, of which 4 were waited for; matrix products, arithmetic and copies ran while one was open for 0% of the time, Pallas kernels for 2%

profile of v5, /device:TPU:8, one launch (start us, length us, event | category | flops | bytes accessed | tf_op | source)
XLA Modules:
  0.0 156.4 jit_solution(6417099412711020677)
XLA Ops:
  0.6 0.1 pad_add_fusion.place
  0.7 1.1 copy-done.2
  1.8 1.6 %shard_map.61 = bf16[640,128]{1,0:T(8,128)(2,1)} custom-call(s32[2]{0:T(128)S(1)} %pad_add_fusion.place, bf16[3,24,4096]{2,1,0:T(8,128)(2,1)S(1)} %bitcast.17), custom_call_target="tpu_custom_call" | custom-call | tf_op jit(solution)/shard_map/pallas_call | solution.py:283
  3.5 16.7 %all-to-all-start = ((bf16[64,5,2,128]{3,2,1,0:T(2,128)(2,1)}), bf16[64,5,2,128]{3,2,1,0:T(2,128)(2,1)S(1)}, u32[]{:S(2)}, u32[]{:S(2)}) async-start(bf16[64,5,2,128]{3,2,1,0:T(2,128)(2,1)} %bitcast.4), calls=%async_computation | async-start | bytes 327680 | tf_op jit(solution)/shard_map/all_to_all | solution.py:298
  20.2 2.0 %shard_map.59 = (f32[192,384]{1,0:T(8,128)S(1)}, f32[192,384]{1,0:T(8,128)S(1)}) custom-call(s32[2]{0:T(128)S(1)} %pad_add_fusion.place, f32[9,9]{1,0:T(8,128)S(1)} %copy-done.3, bf16[3,64,512]{2,1,0:T(8,128)(2,1)S(1)} %bitcast.14, bf16[1536,256]{1,0:T(8,128)(2,1)S(1)} %copy-done.1), custom_call_target="tpu_custom_call" | custom-call | tf_op jit(solution)/shard_map/pallas_call | solution.py:283
  22.2 1.9 %collective-permute-start = (f32[192,384]{1,0:T(8,128)S(1)}, f32[192,384]{1,0:T(8,128)S(1)}, u32[]{:S(2)}, u32[]{:S(2)}) collective-permute-start(f32[192,384]{1,0:T(8,128)S(1)} %get-tuple-element.13), channel_id=1, source_target_pairs={{0,1},{1,0},{2,3},{3,2},{4,5},{5,4},{6,7},{7,6},{8,9},{9,8},{10,11... | collective-permute-start | bytes 884744 | tf_op jit(solution)/shard_map/ppermute | solution.py:306
  24.2 1.5 collective-permute-done.received
  25.8 6.9 %all-to-all-done = bf16[64,5,2,128]{3,2,1,0:T(2,128)(2,1)S(1)} async-done(((bf16[64,5,2,128]{3,2,1,0:T(2,128)(2,1)}), bf16[64,5,2,128]{3,2,1,0:T(2,128)(2,1)S(1)}, u32[]{:S(2)}, u32[]{:S(2)}) %all-to-all-start) | async-done | bytes 163872 | tf_op jit(solution)/shard_map/all_to_all | solution.py:298
  32.7 12.7 %all_to_all.30.weight = bf16[4,192,384]{2,1,0:T(8,128)(2,1)S(1)} all-to-all(bf16[4,192,384]{2,1,0:T(8,128)(2,1)S(1)} %shard_map.60), channel_id=1, replica_groups={{0,2,4,6},{1,3,5,7},{8,10,12,14},{9,11,13,15},{16,18,20,22},{17,19,21,2..., dimensions={0} | all-to-all | bytes 1179648 | tf_op jit(solution)/shard_map/all_to_all | solution.py:298
  45.4 0.9 shard_map.62
  46.2 21.6 %all_to_all.31 = bf16[64,9,2,128]{3,2,1,0:T(2,128)(2,1)S(1)} all-to-all(bf16[64,9,2,128]{3,2,1,0:T(2,128)(2,1)S(1)} %bitcast.18), channel_id=1, replica_groups=mesh['row'=64,'col'=8] {'row'}, dimensions={0} | all-to-all | bytes 589824 | tf_op jit(solution)/shard_map/all_to_all | solution.py:298
  67.8 0.1 shard_map.63
  67.9 19.2 %all_to_all.32 = bf16[64,9,2,128]{3,2,1,0:T(2,128)(2,1)S(1)} all-to-all(bf16[64,9,2,128]{3,2,1,0:T(2,128)(2,1)S(1)} %bitcast.19), channel_id=1, replica_groups=mesh['row'=64,'col'=8] {'row'}, dimensions={0} | all-to-all | bytes 589824 | tf_op jit(solution)/shard_map/all_to_all | solution.py:298
  87.1 1.9 %collective-permute-start.1 = (bf16[1152,128]{1,0:T(8,128)(2,1)S(1)}, bf16[1152,128]{1,0:T(8,128)(2,1)S(1)}, u32[]{:S(2)}, u32[]{:S(2)}) collective-permute-start(bf16[1152,128]{1,0:T(8,128)(2,1)S(1)} %bitcast.10), channel_id=1, source_target_pairs={{0,1},{1,0},{2,3},{3,2},{4,5},{5,4},{6,7},{7,6},{8,9},{9,8},{10,11... | collective-permute-start | bytes 884744 | tf_op jit(solution)/shard_map/ppermute | solution.py:306
  89.0 1.2 shard_map.64.value
  90.2 0.4 collective-permute-done.1.other_in
  90.5 1.0 shard_map.65
  91.6 17.6 %all_to_all.33.pieces = bf16[4,984,128]{2,1,0:T(8,128)(2,1)S(1)} all-to-all(bf16[4,984,128]{2,1,0:T(8,128)(2,1)S(1)} %shard_map.65), channel_id=1, replica_groups={{0,2,4,6},{1,3,5,7},{8,10,12,14},{9,11,13,15},{16,18,20,22},{17,19,21,2..., dimensions={0} | all-to-all | bytes 2015232 | tf_op jit(solution)/shard_map/all_to_all | solution.py:298
  109.2 0.2 shard_map.66.mine
  109.4 2.1 %collective-permute-start.2 = (bf16[1632,128]{1,0:T(8,128)(2,1)S(1)}, bf16[1632,128]{1,0:T(8,128)(2,1)S(1)}, u32[]{:S(2)}, u32[]{:S(2)}) collective-permute-start(bf16[1632,128]{1,0:T(8,128)(2,1)S(1)} %shard_map.66.mine), channel_id=1, source_target_pairs={{0,1},{1,0},{2,3},{3,2},{4,5},{5,4},{6,7},{7,6},{8,9},{9,8},{10,11... | collective-permute-start | bytes 1253384 | tf_op jit(solution)/shard_map/ppermute | solution.py:306
  111.5 1.5 collective-permute-done.2.other
  113.0 13.0 %shard_map.67 = (f32[72,256]{1,0:T(8,128)}, bf16[64,8,768]{2,1,0:T(8,128)(2,1)S(1)}) custom-call(s32[2]{0:T(128)S(1)} %pad_add_fusion.place, bf16[1632,128]{1,0:T(8,128)(2,1)S(1)} %shard_map.66.mine, bf16[1632,128]{1,0:T(8,128)(2,1)S(1)} %collective-permute-done.2.other, bf16[3,64,512]{2,1,0:T(8,128)(2,1)S(1)} %bitcast.15), custom_call_target="tpu_custom_call" | custom-call | tf_op jit(solution)/shard_map/pallas_call | solution.py:283
  126.0 29.0 %all_to_all.34.pieces = bf16[64,8,768]{2,1,0:T(8,128)(2,1)S(1)} all-to-all(bf16[64,8,768]{2,1,0:T(8,128)(2,1)S(1)} %get-tuple-element.21), channel_id=1, replica_groups=mesh['row'=64,'col'=8] {'row'}, dimensions={0} | all-to-all | bytes 1572864 | tf_op jit(solution)/shard_map/all_to_all | solution.py:298
  155.0 1.4 shard_map.68
  (8 shorter events, 0.1 us)
Async XLA Ops:
  0.6 19.6 %copy-start.1 = (bf16[1536,256]{1,0:T(8,128)(2,1)S(1)}, bf16[1536,256]{1,0:T(8,128)(2,1)}, u32[]{:S(2)}) copy-start(bf16[1536,256]{1,0:T(8,128)(2,1)} %probes.1) | copy-start | bytes 2359300
  0.7 1.1 copy-start.2
  3.5 16.7 %copy-start = (bf16[64,3,512]{2,0,1:T(8,128)(2,1)S(1)}, bf16[64,3,512]{2,0,1:T(8,128)(2,1)}, u32[]{:S(2)}) copy-start(bf16[64,3,512]{2,0,1:T(8,128)(2,1)} %param.5) | copy-start | bytes 589828
  3.5 16.7 %copy-start.3 = (f32[9,9]{1,0:T(8,128)S(1)}, f32[9,9]{1,0:T(8,128)}, u32[]{:S(2)}) copy-start(f32[9,9]{1,0:T(8,128)} %gate.3) | copy-start | bytes 976
  3.5 29.2 %all-to-all-start = ((bf16[64,5,2,128]{3,2,1,0:T(2,128)(2,1)}), bf16[64,5,2,128]{3,2,1,0:T(2,128)(2,1)S(1)}, u32[]{:S(2)}, u32[]{:S(2)}) async-start(bf16[64,5,2,128]{3,2,1,0:T(2,128)(2,1)} %bitcast.4), calls=%async_computation | async-start | bytes 327680 | tf_op jit(solution)/shard_map/all_to_all | solution.py:298
  22.2 3.5 %collective-permute-start = (f32[192,384]{1,0:T(8,128)S(1)}, f32[192,384]{1,0:T(8,128)S(1)}, u32[]{:S(2)}, u32[]{:S(2)}) collective-permute-start(f32[192,384]{1,0:T(8,128)S(1)} %get-tuple-element.13), channel_id=1, source_target_pairs={{0,1},{1,0},{2,3},{3,2},{4,5},{5,4},{6,7},{7,6},{8,9},{9,8},{10,11... | collective-permute-start | bytes 884744 | tf_op jit(solution)/shard_map/ppermute | solution.py:306
  87.1 3.5 %collective-permute-start.1 = (bf16[1152,128]{1,0:T(8,128)(2,1)S(1)}, bf16[1152,128]{1,0:T(8,128)(2,1)S(1)}, u32[]{:S(2)}, u32[]{:S(2)}) collective-permute-start(bf16[1152,128]{1,0:T(8,128)(2,1)S(1)} %bitcast.10), channel_id=1, source_target_pairs={{0,1},{1,0},{2,3},{3,2},{4,5},{5,4},{6,7},{7,6},{8,9},{9,8},{10,11... | collective-permute-start | bytes 884744 | tf_op jit(solution)/shard_map/ppermute | solution.py:306
  109.4 3.7 %collective-permute-start.2 = (bf16[1632,128]{1,0:T(8,128)(2,1)S(1)}, bf16[1632,128]{1,0:T(8,128)(2,1)S(1)}, u32[]{:S(2)}, u32[]{:S(2)}) collective-permute-start(bf16[1632,128]{1,0:T(8,128)(2,1)S(1)} %shard_map.66.mine), channel_id=1, source_target_pairs={{0,1},{1,0},{2,3},{3,2},{4,5},{5,4},{6,7},{7,6},{8,9},{9,8},{10,11... | collective-permute-start | bytes 1253384 | tf_op jit(solution)/shard_map/ppermute | solution.py:306
